TPU v7x, 128 devices: a whole 4x4x4 slice. The times are simulated.
128 devices in a mesh: rep: 1, dp: 128 (over x, y, z, core).
Axes of the slice: x: 4, y: 4, z: 4, core: 2. Of those that a mesh axis runs over, the one named last changes fastest.
Arguments:
- x: bfloat16 [128, 1024, 1024], P(('rep', 'dp'))
- dy: bfloat16 [128, 1024, 1024], P(('rep', 'dp'))
- w_gate: bfloat16 [2, 1024, 3200], replicated
- w_up: bfloat16 [2, 1024, 3200], replicated
- w_down: bfloat16 [2, 3200, 1024], replicated
- m_w_gate: float32 [2, 1024, 3200], P(None, 'dp')
- m_w_up: float32 [2, 1024, 3200], P(None, 'dp')
- m_w_down: float32 [2, 3200, 1024], P(None, 'dp')
- v_w_gate: float32 [2, 1024, 3200], P(None, 'dp')
- v_w_up: float32 [2, 1024, 3200], P(None, 'dp')
- v_w_down: float32 [2, 3200, 1024], P(None, 'dp')
Outputs:
- output 1: bfloat16 [2, 1024, 3200], P('rep')
- output 2: bfloat16 [2, 1024, 3200], P('rep')
- output 3: bfloat16 [2, 3200, 1024], P('rep')
- output 4: float32 [2, 1024, 3200], P('rep', 'dp')
- output 5: float32 [2, 1024, 3200], P('rep', 'dp')
- output 6: float32 [2, 3200, 1024], P('rep', 'dp')
- output 7: float32 [2, 1024, 3200], P('rep', 'dp')
- output 8: float32 [2, 1024, 3200], P('rep', 'dp')
- output 9: float32 [2, 3200, 1024], P('rep', 'dp')
All inputs are finite; a program needn't handle non-finite values.
Results may differ from a plain program's by a relative error of at most 0.022.
Values are sent between devices in bfloat16 or wider.
A program may use at most 1.5 GiB of HBM per device.

v0:
```python
import jax
import jax.numpy as jnp
from jax import lax

NAMES = ("w_gate", "w_up", "w_down")


def matmul(a, w):
    return jnp.dot(a, w, preferred_element_type=jnp.float32).astype(jnp.bfloat16)


def normed(h):
    wide = h.astype(jnp.float32)
    scale = lax.rsqrt(jnp.mean(wide**2, -1, keepdims=True) + 1e-6)
    return (wide * scale).astype(jnp.bfloat16)


def layer(h, w):
    a = normed(h)
    gate = jnp.dot(a, w["w_gate"], preferred_element_type=jnp.float32)
    up = jnp.dot(a, w["w_up"], preferred_element_type=jnp.float32)
    return h + matmul((jax.nn.silu(gate) * up).astype(jnp.bfloat16), w["w_down"])


def adamw(w, m, v, g):
    m = 0.9 * m + 0.1 * g
    v = 0.95 * v + 0.05 * g * g
    step = m * lax.rsqrt(v + 1e-8) + 0.1 * w
    return (w - 0.02 * step).astype(jnp.bfloat16), m, v


def stack(weights, h):
    for number in range(weights["w_gate"].shape[0]):
        h = layer(h, {name: w[number] for name, w in weights.items()})
    return h


def solution(mesh):
    groups = mesh.shape["rep"]

    def step(x, dy, *arrays):
        weights, m, v = (arrays[i : i + 3] for i in (0, 3, 6))
        x, dy = (t.reshape(groups, -1, *t.shape[1:]) for t in (x, dy))

        def of_a_group(x, dy):
            _, back = jax.vjp(lambda w: stack(w, x), dict(zip(NAMES, weights, strict=True)))
            by_weights = back(dy)[0]
            gradients = [by_weights[name].astype(jnp.float32) for name in NAMES]
            new = [adamw(w.astype(jnp.float32), m, v, g) for w, m, v, g in zip(weights, m, v, gradients, strict=True)]
            return tuple(one[which] for which in range(3) for one in new)

        return tuple(t.reshape(-1, *t.shape[2:]) for t in jax.vmap(of_a_group)(x, dy))

    return step
```

profile of v0, /device:TPU:1, one launch (start us, length us, event | category | flops | bytes accessed | tf_op | source)
XLA Modules:
  0.0 1236.0 jit_solution(12718612048201622728)
XLA Ops:
  9.3 3.9 copy.6
  13.2 10.8 fusion.48
  24.0 15.5 %fusion.46 = f32[1024,3200]{1,0:T(8,128)S(1)} fusion(bf16[2,1024,3200]{2,1,0:T(8,128)(2,1)} %param.5, bf16[1,1024,1024]{2,1,0:T(8,128)(2,1)} %param.4, f32[1024]{0:T(1024)S(1)} %add_rsqrt_fusion), kind=kOutput, calls=%fused_computation.58 | convolution fusion | flops 6714032128 | bytes 21762048 | tf_op jit(solution)/vmap(jvp())/dot_general | solution.py:21
  39.5 6.5 fusion.28
  46.4 12.2 fusion.65
  58.7 14.0 %fusion.38 = f32[1024,3200]{1,0:T(8,128)} fusion(bf16[2,1024,3200]{2,1,0:T(8,128)(2,1)} %param, bf16[1,1024,1024]{1,2,0:T(8,128)(2,1)S(1)} %get-tuple-element.90, f32[1024]{0:T(1024)S(1)} %bitcast.314), kind=kOutput, calls=%fused_computation.50 | convolution fusion | flops 6714032128 | bytes 21762048 | tf_op jit(solution)/vmap(jvp())/dot_general | solution.py:20
  72.8 13.3 %fusion.41 = f32[1024,3200]{1,0:T(8,128)} fusion(bf16[2,1024,3200]{2,1,0:T(8,128)(2,1)} %param.5, bf16[1,1024,1024]{1,2,0:T(8,128)(2,1)S(1)} %get-tuple-element.90, f32[1024]{0:T(1024)S(1)} %bitcast.315), kind=kOutput, calls=%fused_computation.53 | convolution fusion | flops 6714032128 | bytes 21762048 | tf_op jit(solution)/vmap(jvp())/dot_general | solution.py:21
  86.1 9.4 convolution_convert_fusion.1
  98.4 13.4 %fusion.26 = bf16[1024,1024]{0,1:T(8,128)(2,1)S(1)} fusion(bf16[1024,3200]{1,0:T(8,128)(2,1)} %convolution_convert_fusion.1, f32[1024,3200]{1,0:T(8,128)} %fusion.38, bf16[2,1024,3200]{2,1,0:T(8,128)(2,1)} %param.5), kind=kOutput, calls=%fused_computation.34 | convolution fusion | flops 6730547200 | bytes 28311552 | tf_op jit(solution)/vmap(transpose(jvp()))/dot_general | solution.py:21
  111.8 12.1 fusion.8
  124.0 12.0 fusion.67
  138.9 10.7 convolution_convert_fusion
  152.2 14.2 %fusion.4 = f32[3200,1024]{0,1:T(8,128)} fusion(bf16[1024,3200]{1,0:T(8,128)(2,1)S(1)} %convolution_convert_fusion, f32[1024,3200]{1,0:T(8,128)} %copy-done, bf16[1,1024,1024]{2,1,0:T(8,128)(2,1)S(1)} %copy-done.2, f32[1024]{0:T(1024)S(1)} %add_rsqrt_fusion), kind=kOutput, calls=%fused_computation.8 | convolution fusion | flops 6733692928 | bytes 34869248 | tf_op jit(solution)/vmap(transpose(jvp()))/dot_general | solution.py:21
  166.4 18.1 %fusion.12 = f32[3200,1024]{0,1:T(8,128)} fusion(f32[1024,3200]{1,0:T(8,128)} %copy-done, f32[1024,3200]{1,0:T(8,128)} %copy-done.1, bf16[1024,3200]{1,0:T(8,128)(2,1)} %copy-done.17, bf16[1,1024,1024]{2,1,0:T(8,128)(2,1)S(1)} %copy-done.2, f32[1024]{0:T(1024)S(1)} %add_rsqrt_fusion), kind=kOutput, calls=%fused_computation.15 | convolution fusion | flops 6750076928 | bytes 47976448 | tf_op jit(solution)/vmap(transpose(jvp()))/dot_general | solution.py:20
  184.5 13.6 %fusion.79 = f32[3200,1024]{0,1:T(8,128)} fusion(bf16[1024,3200]{1,0:T(8,128)(2,1)} %copy-done.3, bf16[1,1024,1024]{1,2,0:T(8,128)(2,1)} %copy-done.6, f32[1024]{0:T(1024)S(1)} %bitcast.317), kind=kOutput, calls=%fused_computation.91 | convolution fusion | flops 6714032128 | bytes 21762048 | tf_op jit(solution)/vmap(transpose(jvp()))/dot_general | solution.py:20
  198.1 14.9 %fusion.24 = f32[3200,1024]{0,1:T(8,128)} fusion(bf16[1024,3200]{1,0:T(8,128)(2,1)} %convolution_convert_fusion.1, f32[1024,3200]{1,0:T(8,128)} %fusion.38, bf16[1,1024,1024]{1,2,0:T(8,128)(2,1)S(1)} %copy-done.8, f32[1024]{0:T(1024)S(1)} %bitcast.318), kind=kOutput, calls=%fused_computation.33 | convolution fusion | flops 6733692928 | bytes 34869248 | tf_op jit(solution)/vmap(transpose(jvp()))/dot_general | solution.py:21
  213.0 283.7 %all-reduce.17 = (bf16[3200,1024]{0,1:T(8,128)(2,1)}, bf16[3200,1024]{0,1:T(8,128)(2,1)}, bf16[3200,1024]{0,1:T(8,128)(2,1)}, bf16[3200,1024]{0,1:T(8,128)(2,1)}) all-reduce(f32[3200,1024]{0,1:T(8,128)} %fusion.12, f32[3200,1024]{0,1:T(8,128)} %fusion.79, f32[3200,1024]{0,1:T(8,128)} %fusion.4, ...), channel_id=14, replica_groups=mesh['axis_0'=128] {'axis_0'}, use_global_device_ids=true, to_apply=%add.1.clone.clone | all-reduce | flops 13107200 | bytes 78643200
  502.2 13.2 %fusion.128 = f32[1024,3200]{0,1:T(8,128)} fusion(bf16[1024,1024]{0,1:T(8,128)(2,1)S(1)} %copy-done.5, bf16[1024,3200]{1,0:T(8,128)(2,1)} %fusion.28), kind=kOutput, calls=%fused_computation.158 | convolution fusion | flops 6710886400 | bytes 21757952 | tf_op jit(solution)/vmap(transpose(jvp()))/dot_general | solution.py:9
  515.4 15.6 %fusion.30 = f32[3200,1024]{1,0:T(8,128)} fusion(f32[1024,3200]{1,0:T(8,128)} %fusion.41, f32[1024,3200]{1,0:T(8,128)} %fusion.38, bf16[1,1024,1024]{2,1,0:T(8,128)(2,1)S(1)} %copy-done.10), kind=kOutput, calls=%fused_computation.43 | convolution fusion | flops 6730547200 | bytes 41418752 | tf_op jit(solution)/vmap(transpose(jvp()))/dot_general | solution.py:9
  531.1 380.7 %fusion.125 = (f32[1024,32]{0,1:T(8,128)S(1)}, f32[32,1024]{1,0:T(8,128)S(1)}) fusion(f32[1024,3200]{0,1:T(8,128)} %fusion.128, f32[3200,1024]{1,0:T(8,128)} %fusion.30), kind=kCustom, calls=%all-reduce-scatter.2 | all-reduce-scatter fusion | flops 8388609 | bytes 26476544
  924.4 17.3 %collective-permute-start.13 = (bf16[32,1024]{1,0:T(8,128)(2,1)S(1)}, bf16[32,1024]{1,0:T(8,128)(2,1)S(1)}, u32[]{:S(2)}, u32[]{:S(2)}) collective-permute-start(bf16[32,1024]{1,0:T(8,128)(2,1)S(1)} %convert.141), channel_id=1, source_target_pairs={{0,14},{1,15},{2,16},{3,17},{4,18},{5,19},{6,20},{7,21},{8,22},{9,... | collective-permute-start | bytes 196616
  941.8 4.5 collective-permute-start.14
  946.3 4.4 collective-permute-start.15
  950.7 10.0 collective-permute-start.16
  1011.3 5.3 collective-permute-start.30
  1023.2 4.8 collective-permute-start.34
  1069.4 15.6 %concatenate = bf16[921,1024]{1,0:T(8,128)(2,1)S(1)} concatenate(bf16[25,1024]{1,0:T(8,128)(2,1)S(1)} %collective-permute-done.27, bf16[32,1024]{1,0:T(8,128)(2,1)} %collective-permute-done.26, bf16[32,1024]{1,0:T(8,128)(2,1)} %collective-permute-done.25, bf16[32,1024]{1,0:T(8,128)(2,1)} %collective-permute-done.24, bf16[32,1024]{1,0:T(8,128)(2,1)} %collective-permute-done.23, ...), dimensions={0} | concatenate | bytes 3837952
  1085.1 43.4 %concatenate.1 = bf16[1024,921]{0,1:T(8,128)(2,1)} concatenate(bf16[1024,25]{0,1:T(8,128)(2,1)S(1)} %collective-permute-done.55, bf16[1024,32]{0,1:T(8,128)(2,1)} %collective-permute-done.54, bf16[1024,32]{0,1:T(8,128)(2,1)} %collective-permute-done.53, bf16[1024,32]{0,1:T(8,128)(2,1)} %collective-permute-done.52, bf16[1024,32]{0,1:T(8,128)(2,1)} %collective-permute-done.51, ...), dimensions={1} | concatenate | bytes 3837952
  1133.1 67.2 %all-gather.14.cloned.1.call-done = bf16[1,2,3200,1024]{3,1,0,2:T(2,128)(2,1)} async-done(((bf16[1,2,25,1024]{3,1,0,2:T(2,128)(2,1)}), bf16[1,2,3200,1024]{3,1,0,2:T(2,128)(2,1)}) %all-gather.14.cloned.1.call-update) | async-done | bytes 13107216 | tf_op jit(solution)/reshape | solution.py:52
  1200.3 14.4 %copy.11 = bf16[2,3200,1024]{2,1,0:T(8,128)(2,1)} copy(bf16[2,3200,1024]{2,0,1:T(2,128)(2,1)} %bitcast.310) | data formatting | bytes 26214400
  1214.7 6.6 copy.38
  1224.1 4.9 copy.39
  (198 shorter events, 134.8 us)
Async XLA Ops:
  7.2 1125.9 %all-gather.12.cloned.1.call-start = ((), (), s32[]{:S(2)}) async-start(), calls=%async_computation.1 | async-start | bytes 13209600 | tf_op jit(solution)/reshape | solution.py:52
  499.4 633.7 %all-gather.10.cloned.1.call-start = ((), (), s32[]{:S(2)}) async-start(), calls=%async_computation | async-start | bytes 13209600 | tf_op jit(solution)/reshape | solution.py:52
  502.1 698.1 %all-gather.14.cloned.1.call-start = ((), (), s32[]{:S(2)}) async-start(), calls=%async_computation.2 | async-start | bytes 13209600 | tf_op jit(solution)/reshape | solution.py:52
  915.2 26.6 %collective-permute-start.1 = (bf16[32,1024]{1,0:T(8,128)(2,1)S(1)}, bf16[32,1024]{1,0:T(8,128)(2,1)S(1)}, u32[]{:S(2)}, u32[]{:S(2)}) collective-permute-start(bf16[32,1024]{1,0:T(8,128)(2,1)S(1)} %convert.141), channel_id=1, source_target_pairs={{0,2},{1,3},{2,4},{3,5},{4,6},{5,7},{6,8},{7,9},{8,10},{9,11},{10,... | collective-permute-start | bytes 196616
  916.5 29.9 %collective-permute-start.10 = (bf16[32,1024]{1,0:T(8,128)(2,1)S(1)}, bf16[32,1024]{1,0:T(8,128)(2,1)S(1)}, u32[]{:S(2)}, u32[]{:S(2)}) collective-permute-start(bf16[32,1024]{1,0:T(8,128)(2,1)S(1)} %convert.141), channel_id=1, source_target_pairs={{0,11},{1,12},{2,13},{3,14},{4,15},{5,16},{6,17},{7,18},{8,19},{9,... | collective-permute-start | bytes 196616
  917.8 32.9 %collective-permute-start.11 = (bf16[32,1024]{1,0:T(8,128)(2,1)S(1)}, bf16[32,1024]{1,0:T(8,128)(2,1)S(1)}, u32[]{:S(2)}, u32[]{:S(2)}) collective-permute-start(bf16[32,1024]{1,0:T(8,128)(2,1)S(1)} %convert.141), channel_id=1, source_target_pairs={{0,12},{1,13},{2,14},{3,15},{4,16},{5,17},{6,18},{7,19},{8,20},{9,... | collective-permute-start | bytes 196616
  923.1 37.6 %collective-permute-start.12 = (bf16[32,1024]{1,0:T(8,128)(2,1)S(1)}, bf16[32,1024]{1,0:T(8,128)(2,1)S(1)}, u32[]{:S(2)}, u32[]{:S(2)}) collective-permute-start(bf16[32,1024]{1,0:T(8,128)(2,1)S(1)} %convert.141), channel_id=1, source_target_pairs={{0,13},{1,14},{2,15},{3,16},{4,17},{5,18},{6,19},{7,20},{8,21},{9,... | collective-permute-start | bytes 196616
  924.4 37.6 %collective-permute-start.13 = (bf16[32,1024]{1,0:T(8,128)(2,1)S(1)}, bf16[32,1024]{1,0:T(8,128)(2,1)S(1)}, u32[]{:S(2)}, u32[]{:S(2)}) collective-permute-start(bf16[32,1024]{1,0:T(8,128)(2,1)S(1)} %convert.141), channel_id=1, source_target_pairs={{0,14},{1,15},{2,16},{3,17},{4,18},{5,19},{6,20},{7,21},{8,22},{9,... | collective-permute-start | bytes 196616
  941.8 23.9 %collective-permute-start.14 = (bf16[32,1024]{1,0:T(8,128)(2,1)S(1)}, bf16[32,1024]{1,0:T(8,128)(2,1)S(1)}, u32[]{:S(2)}, u32[]{:S(2)}) collective-permute-start(bf16[32,1024]{1,0:T(8,128)(2,1)S(1)} %convert.141), channel_id=1, source_target_pairs={{0,15},{1,16},{2,17},{3,18},{4,19},{5,20},{6,21},{7,22},{8,23},{9,... | collective-permute-start | bytes 196616
  946.3 22.0 %collective-permute-start.15 = (bf16[32,1024]{1,0:T(8,128)(2,1)S(1)}, bf16[32,1024]{1,0:T(8,128)(2,1)S(1)}, u32[]{:S(2)}, u32[]{:S(2)}) collective-permute-start(bf16[32,1024]{1,0:T(8,128)(2,1)S(1)} %convert.141), channel_id=1, source_target_pairs={{0,16},{1,17},{2,18},{3,19},{4,20},{5,21},{6,22},{7,23},{8,24},{9,... | collective-permute-start | bytes 196616
  950.7 21.3 %collective-permute-start.16 = (bf16[32,1024]{1,0:T(8,128)(2,1)S(1)}, bf16[32,1024]{1,0:T(8,128)(2,1)S(1)}, u32[]{:S(2)}, u32[]{:S(2)}) collective-permute-start(bf16[32,1024]{1,0:T(8,128)(2,1)S(1)} %convert.141), channel_id=1, source_target_pairs={{0,17},{1,18},{2,19},{3,20},{4,21},{5,22},{6,23},{7,24},{8,25},{9,... | collective-permute-start | bytes 196616
  960.7 15.1 %collective-permute-start.17 = (bf16[32,1024]{1,0:T(8,128)(2,1)S(1)}, bf16[32,1024]{1,0:T(8,128)(2,1)S(1)}, u32[]{:S(2)}, u32[]{:S(2)}) collective-permute-start(bf16[32,1024]{1,0:T(8,128)(2,1)S(1)} %convert.141), channel_id=1, source_target_pairs={{0,18},{1,19},{2,20},{3,21},{4,22},{5,23},{6,24},{7,25},{8,26},{9,... | collective-permute-start | bytes 196616
  962.0 15.7 %collective-permute-start.18 = (bf16[32,1024]{1,0:T(8,128)(2,1)S(1)}, bf16[32,1024]{1,0:T(8,128)(2,1)S(1)}, u32[]{:S(2)}, u32[]{:S(2)}) collective-permute-start(bf16[32,1024]{1,0:T(8,128)(2,1)S(1)} %convert.141), channel_id=1, source_target_pairs={{0,19},{1,20},{2,21},{3,22},{4,23},{5,24},{6,25},{7,26},{8,27},{9,... | collective-permute-start | bytes 196616
  965.7 13.9 %collective-permute-start.19 = (bf16[32,1024]{1,0:T(8,128)(2,1)S(1)}, bf16[32,1024]{1,0:T(8,128)(2,1)S(1)}, u32[]{:S(2)}, u32[]{:S(2)}) collective-permute-start(bf16[32,1024]{1,0:T(8,128)(2,1)S(1)} %convert.141), channel_id=1, source_target_pairs={{0,20},{1,21},{2,22},{3,23},{4,24},{5,25},{6,26},{7,27},{8,28},{9,... | collective-permute-start | bytes 196616
  968.3 13.2 %collective-permute-start.2 = (bf16[32,1024]{1,0:T(8,128)(2,1)S(1)}, bf16[32,1024]{1,0:T(8,128)(2,1)S(1)}, u32[]{:S(2)}, u32[]{:S(2)}) collective-permute-start(bf16[32,1024]{1,0:T(8,128)(2,1)S(1)} %convert.141), channel_id=1, source_target_pairs={{0,3},{1,4},{2,5},{3,6},{4,7},{5,8},{6,9},{7,10},{8,11},{9,12},{10... | collective-permute-start | bytes 196616
  983.4 12.6 %collective-permute-start.25 = (bf16[32,1024]{1,0:T(8,128)(2,1)S(1)}, bf16[32,1024]{1,0:T(8,128)(2,1)}, u32[]{:S(2)}, u32[]{:S(2)}) collective-permute-start(bf16[32,1024]{1,0:T(8,128)(2,1)S(1)} %convert.141), channel_id=1, source_target_pairs={{0,26},{1,27},{2,28},{3,29},{4,30},{5,31},{6,32},{7,33},{8,34},{9,... | collective-permute-start | bytes 196616
  985.3 13.4 %collective-permute-start.26 = (bf16[32,1024]{1,0:T(8,128)(2,1)S(1)}, bf16[32,1024]{1,0:T(8,128)(2,1)}, u32[]{:S(2)}, u32[]{:S(2)}) collective-permute-start(bf16[32,1024]{1,0:T(8,128)(2,1)S(1)} %convert.141), channel_id=1, source_target_pairs={{0,27},{1,28},{2,29},{3,30},{4,31},{5,32},{6,33},{7,34},{8,35},{9,... | collective-permute-start | bytes 196616
  987.2 13.7 %collective-permute-start.3 = (bf16[32,1024]{1,0:T(8,128)(2,1)S(1)}, bf16[32,1024]{1,0:T(8,128)(2,1)}, u32[]{:S(2)}, u32[]{:S(2)}) collective-permute-start(bf16[32,1024]{1,0:T(8,128)(2,1)S(1)} %convert.141), channel_id=1, source_target_pairs={{0,4},{1,5},{2,6},{3,7},{4,8},{5,9},{6,10},{7,11},{8,12},{9,13},{1... | collective-permute-start | bytes 196616
  990.2 13.5 %collective-permute-start.4 = (bf16[32,1024]{1,0:T(8,128)(2,1)S(1)}, bf16[32,1024]{1,0:T(8,128)(2,1)}, u32[]{:S(2)}, u32[]{:S(2)}) collective-permute-start(bf16[32,1024]{1,0:T(8,128)(2,1)S(1)} %convert.141), channel_id=1, source_target_pairs={{0,5},{1,6},{2,7},{3,8},{4,9},{5,10},{6,11},{7,12},{8,13},{9,14},{... | collective-permute-start | bytes 196616
  998.7 12.6 %collective-permute-start.7 = (bf16[32,1024]{1,0:T(8,128)(2,1)S(1)}, bf16[32,1024]{1,0:T(8,128)(2,1)}, u32[]{:S(2)}, u32[]{:S(2)}) collective-permute-start(bf16[32,1024]{1,0:T(8,128)(2,1)S(1)} %convert.141), channel_id=1, source_target_pairs={{0,8},{1,9},{2,10},{3,11},{4,12},{5,13},{6,14},{7,15},{8,16},{9,17... | collective-permute-start | bytes 196616
  1001.0 15.6 %collective-permute-start.8 = (bf16[32,1024]{1,0:T(8,128)(2,1)S(1)}, bf16[32,1024]{1,0:T(8,128)(2,1)}, u32[]{:S(2)}, u32[]{:S(2)}) collective-permute-start(bf16[32,1024]{1,0:T(8,128)(2,1)S(1)} %convert.141), channel_id=1, source_target_pairs={{0,9},{1,10},{2,11},{3,12},{4,13},{5,14},{6,15},{7,16},{8,17},{9,1... | collective-permute-start | bytes 196616
  1003.7 14.8 %collective-permute-start.9 = (bf16[32,1024]{1,0:T(8,128)(2,1)S(1)}, bf16[32,1024]{1,0:T(8,128)(2,1)}, u32[]{:S(2)}, u32[]{:S(2)}) collective-permute-start(bf16[32,1024]{1,0:T(8,128)(2,1)S(1)} %convert.141), channel_id=1, source_target_pairs={{0,10},{1,11},{2,12},{3,13},{4,14},{5,15},{6,16},{7,17},{8,18},{9,... | collective-permute-start | bytes 196616
  1005.7 15.6 %collective-permute-start.28 = (bf16[1024,32]{0,1:T(8,128)(2,1)}, bf16[1024,32]{0,1:T(8,128)(2,1)}, u32[]{:S(2)}, u32[]{:S(2)}) collective-permute-start(bf16[1024,32]{0,1:T(8,128)(2,1)} %convert.142), channel_id=1, source_target_pairs={{0,1},{1,2},{2,3},{3,4},{4,5},{5,6},{6,7},{7,8},{8,9},{9,10},{10,1... | collective-permute-start | bytes 196616
  1008.2 15.0 %collective-permute-start.29 = (bf16[1024,32]{0,1:T(8,128)(2,1)}, bf16[1024,32]{0,1:T(8,128)(2,1)}, u32[]{:S(2)}, u32[]{:S(2)}) collective-permute-start(bf16[1024,32]{0,1:T(8,128)(2,1)} %convert.142), channel_id=1, source_target_pairs={{0,2},{1,3},{2,4},{3,5},{4,6},{5,7},{6,8},{7,9},{8,10},{9,11},{10,... | collective-permute-start | bytes 196616
  1011.3 16.7 %collective-permute-start.30 = (bf16[1024,32]{0,1:T(8,128)(2,1)}, bf16[1024,32]{0,1:T(8,128)(2,1)}, u32[]{:S(2)}, u32[]{:S(2)}) collective-permute-start(bf16[1024,32]{0,1:T(8,128)(2,1)} %convert.142), channel_id=1, source_target_pairs={{0,3},{1,4},{2,5},{3,6},{4,7},{5,8},{6,9},{7,10},{8,11},{9,12},{10... | collective-permute-start | bytes 196616
  1016.6 13.3 %collective-permute-start.31 = (bf16[1024,32]{0,1:T(8,128)(2,1)}, bf16[1024,32]{0,1:T(8,128)(2,1)}, u32[]{:S(2)}, u32[]{:S(2)}) collective-permute-start(bf16[1024,32]{0,1:T(8,128)(2,1)} %convert.142), channel_id=1, source_target_pairs={{0,4},{1,5},{2,6},{3,7},{4,8},{5,9},{6,10},{7,11},{8,12},{9,13},{1... | collective-permute-start | bytes 196616
  1018.5 13.3 %collective-permute-start.32 = (bf16[1024,32]{0,1:T(8,128)(2,1)}, bf16[1024,32]{0,1:T(8,128)(2,1)}, u32[]{:S(2)}, u32[]{:S(2)}) collective-permute-start(bf16[1024,32]{0,1:T(8,128)(2,1)} %convert.142), channel_id=1, source_target_pairs={{0,5},{1,6},{2,7},{3,8},{4,9},{5,10},{6,11},{7,12},{8,13},{9,14},{... | collective-permute-start | bytes 196616
  1059.6 25.4 %collective-permute-start.50 = (bf16[1024,32]{0,1:T(8,128)(2,1)}, bf16[1024,32]{0,1:T(8,128)(2,1)}, u32[]{:S(2)}, u32[]{:S(2)}) collective-permute-start(bf16[1024,32]{0,1:T(8,128)(2,1)} %convert.142), channel_id=1, source_target_pairs={{0,23},{1,24},{2,25},{3,26},{4,27},{5,28},{6,29},{7,30},{8,31},{9,... | collective-permute-start | bytes 196616
  1061.5 23.5 %collective-permute-start.51 = (bf16[1024,32]{0,1:T(8,128)(2,1)}, bf16[1024,32]{0,1:T(8,128)(2,1)}, u32[]{:S(2)}, u32[]{:S(2)}) collective-permute-start(bf16[1024,32]{0,1:T(8,128)(2,1)} %convert.142), channel_id=1, source_target_pairs={{0,24},{1,25},{2,26},{3,27},{4,28},{5,29},{6,30},{7,31},{8,32},{9,... | collective-permute-start | bytes 196616
  1063.7 21.3 %collective-permute-start.52 = (bf16[1024,32]{0,1:T(8,128)(2,1)}, bf16[1024,32]{0,1:T(8,128)(2,1)}, u32[]{:S(2)}, u32[]{:S(2)}) collective-permute-start(bf16[1024,32]{0,1:T(8,128)(2,1)} %convert.142), channel_id=1, source_target_pairs={{0,25},{1,26},{2,27},{3,28},{4,29},{5,30},{6,31},{7,32},{8,33},{9,... | collective-permute-start | bytes 196616
  1065.6 19.5 %collective-permute-start.53 = (bf16[1024,32]{0,1:T(8,128)(2,1)}, bf16[1024,32]{0,1:T(8,128)(2,1)}, u32[]{:S(2)}, u32[]{:S(2)}) collective-permute-start(bf16[1024,32]{0,1:T(8,128)(2,1)} %convert.142), channel_id=1, source_target_pairs={{0,26},{1,27},{2,28},{3,29},{4,30},{5,31},{6,32},{7,33},{8,34},{9,... | collective-permute-start | bytes 196616
  1067.5 17.6 %collective-permute-start.54 = (bf16[1024,32]{0,1:T(8,128)(2,1)}, bf16[1024,32]{0,1:T(8,128)(2,1)}, u32[]{:S(2)}, u32[]{:S(2)}) collective-permute-start(bf16[1024,32]{0,1:T(8,128)(2,1)} %convert.142), channel_id=1, source_target_pairs={{0,27},{1,28},{2,29},{3,30},{4,31},{5,32},{6,33},{7,34},{8,35},{9,... | collective-permute-start | bytes 196616
  (57 other events, 2442.6 us)
Sparse Core Ops, SparseCore 0:
  499.5 86.4 all-gather.11
  589.0 92.6 all-gather.9
  1131.5 68.7 all-gather.13
where the time goes:
time: 1250 us; the launch traced here: 1240 us
  blocking collectives  664 us (53%)
  matrix products  201 us (16%)
  starting transfers between devices  155 us (12%)
  local copies, waits for them, and re-layouts  104 us (8%)
  waiting for transfers between devices  68.7 us (5%)
  other arithmetic  27.7 us (2%)
  between operations  14.9 us (1%)
    unnamed x2, blocking collectives  664 us
    unnamed x56, starting transfers between devices  155 us
    unnamed x71, local copies, waits for them, and re-layouts  101 us
    dot_general x5, matrix products, layer(): up = jnp.dot(a, w['w_up'], preferred_element_type=jnp.float32)  71.3 us
    dot_general x5, matrix products, layer(): gate = jnp.dot(a, w['w_gate'], preferred_element_type=jnp.float32)  68.4 us
    reshape x3, waiting for transfers between devices, step(): t.reshape(-1, *t.shape[2:])  67.2 us
    dot_general x5, matrix products, matmul(): jnp.dot(a, w, preferred_element_type=jnp.float32).astype(jnp.bfloat16)  61.2 us
  transfers between devices with their start and end apart: 59, of which 2 were waited for; matrix products, arithmetic and copies ran while one was open for 39% of the time, Pallas kernels for 0%

commit v1 on v0

v1 whole, which is shorter than its diff:
```python
import functools

import jax
import jax.numpy as jnp
from jax import lax
from jax.experimental import pallas as pl
from jax.experimental.pallas import tpu as pltpu
from jax.sharding import PartitionSpec as P

MESH = pl.DeviceIdType.MESH
TWO = 2
BF, F32 = jnp.bfloat16, jnp.float32
LAYERS, D, FF, TOK = 2, 1024, 3200, 1024
LANES, ROWS, OCT = 128, 16, 8
PARTS, CHIPS, HALF = 6, 64, 32
TILE, TILES = 256, 13
TB = 2 * CHIPS
ORDER = ("x1", "y1", "z1", "x0", "y0", "z0")
GROUP, GROUPS, ROWS_GROUP = 8, 16, 200
PAIR = 2 * ROWS_GROUP
UNITS = ROWS_GROUP // ROWS
OWN_ROWS = ROWS_GROUP // GROUP
WIN = 32

G1, D1, D0, G0, NW = 0, 4, 6, 8, 12
SHORT = (0, 3)
NS = 2
OWN_SLOT = (0, 1, 2, 0, 1, 2, 0, 3, 2, 0, 1, 2)
OWN_SLOTS = 4
NRS, NDD, NX = 4, 2, 4

T_F, T_FN, T_L1, T_DOWN1, T_NORM, T_DOWN0, T_B0, T_TAIL = 0, 13, 14, 40, 44, 45, 49, 62
START = (21, 27, 33, 39, 43, 44, 48, 49, 52, 55, 58, 61)
SHORT_START = (50, 45)
OFF = (0, 2, 4, 6, 7, 8, 9, 10, 11, 12)
DX = ((61, 63, 65), (56, 58, 60))
AGS = (33, 39, 45, 51, 60, 61, 65, 66, 64, 67, 70, 73)
SHORT_AGS = (65, 60)
AGO = (0, 2, 4, 6, 8, 10, 13, 16)
TICKS = 90


def div(a, b):
    return a // b if isinstance(a, int) else lax.div(a, jnp.int32(b))


def mod(a, b):
    return a % b if isinstance(a, int) else lax.rem(a, jnp.int32(b))


def base_of(x, y, z):
    r = 0
    for d in ORDER:
        v = {"x": x, "y": y, "z": z}[d[0]]
        r = TWO * r + gray(v, d)
    return r


def gray(v, d):
    h, l = div(v, 2), mod(v, 2)
    return h if d.endswith("1") else h + l - TWO * h * l


CHIP_AT = [None] * CHIPS
for _n in range(CHIPS):
    CHIP_AT[base_of(_n // 16, _n // 4 % 4, _n % 4)] = _n


def rotl(u, p):
    return mod(u * TWO**p, CHIPS) + div(u * TWO**p, CHIPS)


def rotr(u, p):
    return rotl(u, (PARTS - p) % PARTS)


def off_of(i):
    return pl.multiple_of(jnp.maximum(TILE * i - LANES, 0), LANES)


def aligned(start, size, to=None):
    return pl.ds(pl.multiple_of(start, to or size), size)


def dot(a, b, cb=0):
    return lax.dot_general(a, b, (((1,), (cb,)), ((), ())), preferred_element_type=F32)


def pick(w, values):
    r = values[0]
    for q, v in enumerate(values):
        if q:
            r = jnp.where(w == q, v, r)
    return r


def adam(w, m, v, g):
    m = 0.9 * m + 0.1 * g
    v = 0.95 * v + 0.05 * g * g
    step = m * lax.rsqrt(v + 1e-8) + 0.1 * w
    return (w - 0.02 * step).astype(BF).astype(F32), m, v


def rms_scale(squares):
    return lax.rsqrt(squares * (1.0 / D) + 1e-6)


def lanes(q):
    return slice(LANES * q, LANES * q + LANES)


def step_kernel(
    x, dy, w_gate, w_up, w_down, m_g, m_u, m_d, v_g, v_u, v_d,
    ag, agm, hidt, a0t, gu0, om_g, om_u, om_d, ov_g, ov_u, ov_d,
    acts, at, da, wgu, wdb, dgb, dub, hidb, hts, htb, wr_g, wr_u, wr_d,
    own, d2d, acc, r1, r2, r3, r4, r5, r6, s1, s2, s3, s4, s5, s6,
    d2dm, accm, q1, q2, q3, q4, q5, q6, t1, t2, t3, t4, t5, t6,
    gfin, xg, wsend, wrecv, fin, g_d, gx, ws_d, wx,
    lsem, wsem, gsem, hsem, htsem, d2s, d2r, ssem, rsem, xs, xr, wsm, wrm, agl, ags, agr, dags, dagr, dxs, dxr, d2c, rcred,
):
    dp = lax.axis_index("dp")
    c = mod(dp, 2)
    pos = {"x": div(dp, 32), "y": mod(div(dp, 8), 4), "z": mod(div(dp, 2), 4)}
    other = dp + 1 - TWO * c
    j_me = pos["z"] * TWO + c

    def device(x, y, z, core):
        return ((x * 4 + y) * 4 + z) * TWO + core

    def partner(d):
        o = pos[d[0]]
        return device(**(pos | {d[0]: 3 - o if d.endswith("1") else o + 1 - TWO * mod(o, 2)}), core=c)

    bits = [gray(pos[d[0]], d) for d in ORDER]
    partners = [partner(d) for d in ORDER]
    rot = [rotl(base_of(**pos), p) for p in range(PARTS)]

    def group_dev(j):
        return device(pos["x"], pos["y"], div(j, 2), mod(j, 2))

    def rcopy(src, dst, ss, rs, dev):
        return pltpu.make_async_remote_copy(src_ref=src, dst_ref=dst, send_sem=ss, recv_sem=rs, device_id={"dp": dev}, device_id_type=MESH)

    def signal(sem, dev):
        pl.semaphore_signal(sem, inc=1, device_id={"dp": dev}, device_id_type=MESH)

    copy = pltpu.make_async_copy

    barrier = pltpu.get_barrier_semaphore()
    for r in range(1, GROUP):
        signal(barrier, group_dev(mod(j_me + r, GROUP)))
    far = [q for d, q in zip(ORDER, partners) if d[0] != "z"]
    for q in far:
        signal(barrier, q)

    def weights(layer, i, b, gate_up=True):
        o = pl.ds(off_of(i), TILE)
        down = [copy(w_down.at[layer, o], wdb.at[b], wsem.at[b, 2])]
        if not gate_up:
            return down
        return down + [copy(w.at[layer, :, o], wgu.at[TWO * b + k], wsem.at[b, k]) for k, w in enumerate((w_gate, w_up))]

    def saved(i, b):
        return weights(0, i, b, False) + [copy(gu0.at[i], da.at[pl.ds(b * TWO * TB, TWO * TB)], gsem.at[b])]

    def stream(make, i, b):
        for cp in make(i, b):
            cp.wait()

        @pl.when(i + 1 < TILES)
        def _():
            for cp in make(i + 1, 1 - b):
                cp.start()

    def halves(fn):
        def chunk(k, _):
            fn(k, aligned(k * (TOK // TWO), TOK // TWO))
            return 0

        lax.fori_loop(0, 2, chunk, 0)

    def as_blocks(v):
        return v.reshape(v.shape[0] // ROWS, ROWS, LANES)

    def get_da(q, rows, n):
        return da[pl.ds(q * CHIPS + div(rows, ROWS), n // ROWS)].reshape(n, LANES)

    def sigmoid(v):
        return 1.0 / (1.0 + jnp.exp(-v))

    def through_act(gate, up, dhid):
        sg = sigmoid(gate)
        s = gate * sg
        return s, dhid * up * (sg * (1.0 + gate * (1.0 - sg))), dhid * s

    def counts(i):
        return (lax.broadcasted_iota(jnp.int32, (TOK // TWO, TILE), 1) < LANES) | (i > 0)

    def add_products(terms):
        def part(n, _):
            total = sum(dot(a[...], *rhs(n)) for a, rhs in terms)
            for q in range(TWO):
                o = pl.ds((TWO * n + q) * CHIPS, CHIPS)
                da[o] = da[o] + as_blocks(total[:, lanes(q)])
            return 0

        lax.fori_loop(0, D // TILE, part, 0)

    def hid_write(layer, i, b, q):
        o = pl.multiple_of(off_of(i) + LANES * q, LANES)
        return copy(hts.at[b, lanes(q)], hidt.at[layer, pl.ds(o, LANES)], hsem.at[b, q])

    def put_hidden(layer, i, b):
        for q in range(TWO):

            @pl.when(i >= 2 + q)
            def _():
                hid_write(layer, i - 2, b, q).wait()

        hts[b] = hidb[...].T
        for q in range(TWO):

            @pl.when(i >= q)
            def _():
                hid_write(layer, i, b, q).start()

    def hidden_out(layer):
        for i in (TILES - 2, TILES - 1):
            for q in range(TWO):
                hid_write(layer, i, i % TWO, q).wait()

    def gu_out(i, b):
        return copy(acc.at[pl.ds(b * TWO * TB, TWO * TB)], gu0.at[i], gsem.at[b])

    def tick_f(i):
        b = mod(i, 2)
        stream(functools.partial(weights, 0), i, b)

        @pl.when(i >= 2)
        def _():
            gu_out(i - 2, b).wait()

        def chunk(k, rows):
            gate = dot(acts[1, rows], wgu[TWO * b])
            up = dot(acts[1, rows], wgu[TWO * b + 1])
            hidb[rows] = jnp.where(counts(i), gate * sigmoid(gate) * up, 0.0).astype(BF)
            for m, t in enumerate((gate, up)):
                for q in range(TWO):
                    acc[pl.ds((TWO * b + m) * TB + q * CHIPS + k * HALF, HALF)] = as_blocks(t[:, lanes(q)])

        halves(chunk)
        gu_out(i, b).start()
        add_products([(hidb, lambda n: (wdb[b, :, aligned(n * TILE, TILE)],))])
        put_hidden(0, i, b)

    def transpose_in():
        def part(k, _):
            t = acts[1, :, aligned(k * LANES, LANES)].T
            for q in range(OCT):
                n = k * OCT + q
                at[aligned(base_of(div(n, 16), mod(div(n, 4), 4), mod(n, 4)) * ROWS, ROWS)] = t[q * ROWS : (q + 1) * ROWS]
            return 0

        lax.fori_loop(0, D // LANES, part, 0)

    def by_rows(fn):
        def chunk(k, _):
            fn(k * LANES, aligned(k * LANES, LANES))
            return 0

        lax.fori_loop(0, TOK // LANES, chunk, 0)

    def norm_in(_, rows):
        h = acts[2, rows].astype(F32)
        acts[1, rows] = (h * rms_scale(jnp.sum(h * h, -1, keepdims=True))).astype(BF)

    def tick_fn():
        for b in range(TWO):
            gu_out(TILES - 2 + (b + TILES) % TWO, b).wait()

        def chunk(r, rows):
            o = jnp.concatenate([get_da(q, r, LANES) for q in range(OCT)], 1).astype(BF).astype(F32)
            acts[2, rows] = (acts[2, rows].astype(F32) + o).astype(BF)
            for q in range(OCT):
                da[pl.ds(q * CHIPS + div(r, ROWS), OCT)] = jnp.zeros((OCT, ROWS, LANES), F32)
            norm_in(r, rows)

        by_rows(chunk)
        a0t_out.wait()
        transpose_in()
        hidden_out(0)

    def tick_a(i):
        b = mod(i, 2)
        stream(functools.partial(weights, 1), i, b)

        def chunk(_, rows):
            gate = dot(acts[1, rows], wgu[TWO * b])
            up = dot(acts[1, rows], wgu[TWO * b + 1])
            dhid = dot(acts[0, rows], wdb[b], 1).astype(BF).astype(F32)
            s, dgate, dup = through_act(gate, up, dhid)
            hidb[rows] = (s * up).astype(BF)
            dgb[rows] = jnp.where(counts(i), dgate, 0.0).astype(BF)
            dub[rows] = jnp.where(counts(i), dup, 0.0).astype(BF)

        halves(chunk)

    def grads_gate_up(i, slot, layer):
        first = i == 0
        part = slot * PARTS + TWO * mod(i + 2, 3)
        pa = jnp.where(first, OWN_SLOTS * PARTS + TWO * layer, part)
        pb = jnp.where(first, slot * PARTS, part + 1)

        def chunk(k, rows):
            blocks = pl.ds(k * HALF, HALF)
            lhs = at[rows]
            for mat, src in enumerate((dgb, dub)):
                r = dot(lhs, src[...]).astype(BF)
                for q, p in enumerate((pa, pb)):
                    own[mat, p, blocks] = as_blocks(r[:, lanes(q)])

        halves(chunk)

    def wave_in_layer(i):
        return div(jnp.maximum(i - 1, 0), 3)

    def tick_b(i):
        b = mod(i, 2)
        grads_gate_up(i, mod(wave_in_layer(i), 3), 1)
        add_products([(t, lambda n, m=m: (wgu[TWO * b + m, aligned(n * TILE, TILE)], 1)) for m, t in enumerate((dgb, dub))])
        put_hidden(1, i, b)

    def hid_load(layer, r):
        return copy(hidt.at[layer, aligned(PAIR * r, PAIR, ROWS)], htb.at[mod(r, 2)], htsem.at[mod(r, 2)])

    def tick_down(k, layer):
        def iteration(r, _):
            hid_load(layer, r).wait()

            @pl.when(r + 1 < OCT)
            def _():
                hid_load(layer, r + 1).start()

            slots = [jnp.where(layer == 1, OWN_SLOT[D1 + q], OWN_SLOT[D0 + q]) * PARTS for q in range(TWO)]
            res = dot(htb[mod(r, 2)], acts[1 - layer])
            for gg in range(TWO):
                g = TWO * r + gg
                at_xy = base_of(div(g, 4), mod(g, 4), 0)
                for lt in range(OCT):
                    place = at_xy + base_of(0, 0, lt % 4)
                    mine = res[gg * ROWS_GROUP : (gg + 1) * ROWS_GROUP, lanes(lt)]
                    for u in range(UNITS):
                        own[lt // 4, slots[u // PARTS] + u % PARTS, place] = mine[ROWS * u : ROWS * u + ROWS].astype(BF)
                    last = jnp.concatenate([mine[ROWS * UNITS :], jnp.zeros((OCT, LANES), F32)], 0)
                    own[lt // 4, OWN_SLOTS * PARTS + TWO * layer + 1, place] = last.astype(BF)
            return 0

        lax.fori_loop(TWO * k, TWO * k + 2, iteration, 0)

    def tick_norm():
        def chunk(r, rows):
            h = acts[2, rows].astype(F32)
            g = jnp.concatenate([get_da(q, r, LANES) for q in range(OCT)], 1).astype(BF).astype(F32)
            scale = rms_scale(jnp.sum(h * h, -1, keepdims=True))
            back = scale * scale * scale * jnp.sum(h * g, -1, keepdims=True) * (1.0 / D)
            dh = (g * scale - h * back).astype(BF).astype(F32)
            acts[1, rows] = (acts[0, rows].astype(F32) + dh).astype(BF)

        by_rows(chunk)

    def tick_back0(i):
        b = mod(i, 2)
        stream(saved, i, b)

        def chunk(k, rows):
            dhid = dot(acts[1, rows], wdb[b], 1).astype(BF).astype(F32)
            gate, up = (
                jnp.concatenate([get_da(4 * b + TWO * m + q, k * (TOK // TWO), TOK // TWO) for q in range(TWO)], 1) for m in range(TWO)
            )
            _, dgate, dup = through_act(gate, up, dhid)
            dgb[rows] = dgate.astype(BF)
            dub[rows] = dup.astype(BF)

        halves(chunk)
        grads_gate_up(i, pick(wave_in_layer(i), OWN_SLOT[G0:]), 0)

    a0t_out = copy(at, a0t, lsem.at[0])
    a0t_in = copy(a0t, at, lsem.at[0])

    def compute(t):
        def between(lo, hi, fn):
            @pl.when((t >= lo) & (t < hi))
            def _():
                fn(t - lo)

        between(T_F, T_FN, tick_f)

        @pl.when(t == T_FN)
        def _():
            for cp in weights(1, 0, 0):
                cp.start()
            tick_fn()
            loads[1].wait()

        @pl.when((t >= T_L1) & (t < T_DOWN1) & (mod(t, 2) == T_L1 % TWO))
        def _():
            tick_a(div(t - T_L1, 2))

        @pl.when((t >= T_L1) & (t < T_DOWN1) & (mod(t, 2) != T_L1 % TWO))
        def _():
            tick_b(div(t - T_L1, 2))

        @pl.when(t == T_DOWN1 - 1)
        def _():
            hid_load(1, 0).start()
            a0t_in.start()

        @pl.when(t == T_DOWN1)
        def _():
            hidden_out(1)

        @pl.when(((t >= T_DOWN1) & (t < T_NORM)) | ((t >= T_DOWN0) & (t < T_B0)))
        def _():
            layer = jnp.where(t < T_NORM, 1, 0)
            tick_down(t - jnp.where(t < T_NORM, T_DOWN1, T_DOWN0), layer)

        @pl.when(t == T_NORM)
        def _():
            hid_load(0, 0).start()
            tick_norm()
            for cp in saved(0, 0):
                cp.start()
            a0t_in.wait()

        between(T_B0, T_TAIL, tick_back0)

    def L(j):
        return 2 ** (PARTS - j)

    starts = [[div(r, L(j)) * L(j) for j in range(PARTS + 1)] for r in rot]

    def kept(p, j):
        return starts[p][j]

    def lag_start(makers):
        last = None
        for make in makers:
            cp = make()
            if last is not None:
                last.start()
            last = cp
        last.start()

    class Full:
        parts = tuple(range(PARTS))
        accumulated, received, sent, crossed, ag_ref = acc, (None, r1, r2, r3, r4, r5, r6), (None, s1, s2, s3, s4, s5, s6), d2d, ag

        def __init__(self, w):
            self.w, self.id, self.r, self.s, self.f = w, w, mod(w, NRS), mod(w, NDD), mod(w, NX)
            self.own = pick(w, OWN_SLOT) * PARTS

    class Short:
        parts = SHORT
        accumulated, received, sent, crossed, ag_ref = accm, (None, q1, q2, q3, q4, q5, q6), (None, t1, t2, t3, t4, t5, t6), d2dm, agm

        def __init__(self, w):
            self.w, self.id, self.r, self.s, self.f = w, NW + w, w, w, NX + w
            self.own = OWN_SLOTS * PARTS + TWO * w

    def sems(v):
        return (v.r, v.s) if isinstance(v, Full) else (NRS + v.r, NDD + v.s)

    def crossing(v):
        s = sems(v)[1]
        return rcopy(own.at[1 - c, pl.ds(v.own, len(v.parts))], v.crossed.at[v.s], d2s.at[s], d2r.at[s], other)

    def stage_all(v, j):
        s = sems(v)[0]
        return rcopy(v.sent[j].at[v.r], v.received[j].at[v.r], ssem.at[s, j - 1], rsem.at[s, j - 1], other)

    def stage_one(v, j, k):
        s = sems(v)[0]
        to = partners[(v.parts[k] + j - 1) % PARTS]
        return rcopy(v.sent[j].at[v.r, k], v.received[j].at[v.r, k], ssem.at[s, j - 1], rsem.at[s, j - 1], to)

    def acc_at(v, k):
        return (v.r * len(v.parts) + k) * HALF

    def rs0(v):
        if isinstance(v, Full):

            @pl.when(v.w >= NDD)
            def _():
                pl.semaphore_wait(d2c.at[v.s], 1)

        crossing(v).start()

    def rs1(v):
        crossing(v).wait_recv()
        if isinstance(v, Full):

            @pl.when(v.w >= NRS)
            def _():
                pl.semaphore_wait(rcred.at[v.r], len(partners))

        def make(k):
            p = v.parts[k]
            b = bits[p]
            lv, kp = (1 - b) * TWO ** (PARTS - 1 - p), b * TWO ** (PARTS - 1 - p)
            def some(g, _):
                at_g = rotr(g * OCT, p)
                for i in range(OCT):
                    u = at_g + rotr(i, p)
                    both = [own[c, v.own + k, o + u].astype(F32) + v.crossed[v.s, k, o + u].astype(F32) for o in (lv, kp)]
                    v.sent[1][v.r, k, g * OCT + i] = both[0].astype(BF)
                    v.accumulated[acc_at(v, k) + g * OCT + i] = both[1]
                return 0

            lax.fori_loop(0, HALF // OCT, some, 0)
            return stage_one(v, 1, k)

        lag_start([functools.partial(make, k) for k in range(len(v.parts))])
        crossing(v).wait_send()
        if isinstance(v, Full):

            @pl.when(v.w + NDD < NW)
            def _():
                signal(d2c.at[v.s], other)

    def rsj(j, v):
        stage_all(v, j - 1).wait_recv()
        n = L(j)
        ch = min(n, OCT)

        def make(k):
            p = v.parts[k]
            b = bits[(p + j - 1) % PARTS]
            o = acc_at(v, k) + kept(p, j - 1) - kept(p, 1)
            for i in range(0, n, ch):
                lv, kp = (1 - b) * n + i, b * n + i
                both = [v.accumulated[pl.ds(o + h, ch)] + v.received[j - 1][v.r, k, pl.ds(h, ch)].astype(F32) for h in (lv, kp)]
                v.sent[j][v.r, k, pl.ds(i, ch)] = both[0].astype(BF)
                v.accumulated[pl.ds(o + kp, ch)] = both[1]
            return stage_one(v, j, k)

        lag_start([functools.partial(make, k) for k in range(len(v.parts))])

    def is_down(w):
        return (w >= D1) & (w < G0)

    def exchange(v):
        return rcopy(gfin.at[v.f, 1 - c], xg.at[v.id], xs.at[v.f], xr.at[v.id], other)

    def rs7(v):
        stage_all(v, PARTS).wait_recv()
        for k, p in enumerate(v.parts):
            g = v.accumulated[acc_at(v, k) + rot[p] - kept(p, 1)] + v.received[PARTS][v.r, k, 0].astype(F32)
            g = g.astype(BF).astype(F32)
            for h in range(TWO):
                gfin[v.f, h, k] = g[OCT * h : OCT * h + OCT]
        for j in range(1, PARTS + 1):
            stage_all(v, j).wait_send()
        if isinstance(v, Short):
            g_d[v.w, ROWS * UNITS : ROWS * UNITS + OCT] = gfin[v.f, 0, 1]
            exchange(v).start()
            return

        @pl.when(v.w + NRS < NW)
        def _():
            for q in partners:
                signal(rcred.at[v.r], q)

        @pl.when(is_down(v.w))
        def _():
            for p in range(PARTS):
                for h in range(TWO):
                    g_d[jnp.where(v.w < D0, 1, 0), aligned((mod(v.w, 2) * PARTS + p) * ROWS + OCT * h, OCT)] = gfin[v.f, h, p]

        @pl.when(~is_down(v.w))
        def _():
            exchange(v).start()

    def adam_tile(layer, col, v, k):
        cols = aligned(col, LANES)
        mine, theirs = gfin[v.f, c, k], xg[v.id, k]
        for mat, (wr, om, ov) in enumerate(((wr_g, om_g, ov_g), (wr_u, om_u, ov_u))):
            g = jnp.where(c == mat, mine, theirs)
            wn, mn, vn = adam(wr[layer, :, cols].astype(F32), om[layer, :, cols], ov[layer, :, cols], g)
            om[layer, :, cols] = mn
            ov[layer, :, cols] = vn
            wsend[v.f, mat, k] = wn

    def w_exchange(v):
        return rcopy(wsend.at[v.f, 1 - c], wrecv.at[v.id], wsm.at[v.f], wrm.at[v.id], other)

    def unless_down(fn):
        def run(v):
            if isinstance(v, Short):
                fn(v)
            else:

                @pl.when(~is_down(v.w))
                def _():
                    fn(v)

        run.__name__ = fn.__name__
        return run

    @unless_down
    def rs8(v):
        exchange(v).wait_recv()
        if isinstance(v, Short):
            adam_tile(v.w, 0, v, 0)
            for mat in range(TWO):
                for k in range(1, PARTS):
                    wsend[v.f, mat, k] = jnp.zeros((OCT, LANES), F32)
        else:
            layer = jnp.where(v.w < G0, 1, 0)
            for k in range(PARTS):
                adam_tile(layer, LANES + PARTS * LANES * (v.w - jnp.where(v.w < G0, 0, G0)) + LANES * k, v, k)
        exchange(v).wait_send()
        w_exchange(v).start()

    @unless_down
    def rs9(v):
        w_exchange(v).wait_recv()
        for k in range(PARTS if isinstance(v, Full) else 1):
            mine, theirs = wsend[v.f, c, k], wrecv[v.id, k]
            fin[v.id, k] = jnp.concatenate([jnp.where(c == 0, mine, theirs), jnp.where(c == 0, theirs, mine)], 0).astype(BF)
        w_exchange(v).wait_send()

    def window(j):
        return div(OWN_ROWS * j, OCT) * OCT

    def to_group(k, layer, src, dst):
        for r in range(1, GROUP):
            j = mod(j_me + r, GROUP)
            rcopy(src(j), dst.at[layer, j_me], dxs.at[k, layer], dxr.at[k, layer], group_dev(j)).start()

    def from_group(k, layer, dst):
        seven = dst.at[layer, pl.ds(0, GROUP - 1)]
        cp = rcopy(seven, seven, dxs.at[k, layer], dxr.at[k, layer], other)
        cp.wait_recv()
        cp.wait_send()

    def dx1(layer):
        def src(j):
            return g_d.at[layer, aligned(window(j), WIN, OCT)]

        to_group(0, layer, src, gx)
        gx[layer, j_me] = g_d[layer, aligned(window(j_me), WIN, OCT)]

    def dx2(layer):
        from_group(0, layer, gx)
        shift = mod(OWN_ROWS * j_me, OCT)
        row = lax.broadcasted_iota(jnp.int32, (WIN, LANES), 0)
        valid = (row >= shift) & (row < shift + OWN_ROWS)
        def tile(lt, _):
            cols = aligned(lt * LANES, LANES)
            m, s = (pltpu.roll(t[layer, :, cols], shift, 0) for t in (om_d, ov_d))
            wn, mn, vn = adam(wr_d[layer, :, cols].astype(F32), m, s, gx[layer, TWO * mod(lt, 4) + div(lt, 4)])
            for o, t in ((om_d, mn), (ov_d, vn)):
                o[layer, :, cols] = pltpu.roll(t, mod(WIN - shift, WIN), 0)
            ws_d[layer, lt] = jnp.where(valid, wn, 0.0)
            return 0

        lax.fori_loop(0, OCT, tile, 0)

        def src(j):
            return ws_d.at[layer, 4 * mod(j, 2) + div(j, 2)]

        to_group(1, layer, src, wx)
        wx[layer, j_me] = ws_d[layer, 4 * c + pos["z"]]

    def dx3(layer):
        from_group(1, layer, wx)
        octets = [None] * (TWO * UNITS + 2)
        for j in range(GROUP):
            for k in range(WIN // OCT):
                o, t = window(j) // OCT + k, wx[layer, j, OCT * k : OCT * k + OCT]
                octets[o] = t if octets[o] is None else octets[o] + t
        octets[-1] = jnp.zeros((OCT, LANES), F32)
        for u in range(UNITS + 1):
            block = jnp.concatenate(octets[TWO * u : TWO * u + 2], 0).astype(BF)
            if u < UNITS:
                fin[jnp.where(layer == 1, D1, D0) + u // PARTS, u % PARTS] = block
            else:
                fin[NW + layer, 1] = block

    def part_of(v):
        return v.ag_ref.at[v.w, c]

    def ag1(v):
        for k, p in enumerate(v.parts):
            src, dst = fin.at[v.id, k], part_of(v).at[k, rot[p]]
            copy(src, dst, agl.at[v.id]).start()
            rcopy(src, dst, ags.at[v.id], agr.at[v.id, 0], partners[(p + PARTS - 1) % PARTS]).start()
            rcopy(src, dst, dags.at[v.id], dagr.at[v.id], other).start()

    def agk(k, v):
        n = 2 ** (k - 2)
        mine = part_of(v)
        if k == 2:
            copy(fin.at[v.id, pl.ds(0, len(v.parts))], mine.at[:, 0], agl.at[v.id]).wait()
        came = mine.at[:, pl.ds(0, n)]
        rcopy(came, came, ags.at[v.id], agr.at[v.id, k - 2], other).wait_recv()
        j = PARTS + 1 - k
        for q, p in enumerate(v.parts):
            if k <= PARTS:
                h = mine.at[q, pl.ds(kept(p, j), TWO * n)]
                rcopy(h, h, ags.at[v.id], agr.at[v.id, k - 1], partners[(p + j - 1) % PARTS]).start()
            g = mine.at[q, pl.ds(kept(p, j) + (1 - bits[(p + j) % PARTS]) * n, n)]
            rcopy(g, g, dags.at[v.id], dagr.at[v.id], other).start()

    def ag_end(v):
        most = part_of(v).at[:, pl.ds(0, CHIPS - 1)]
        rcopy(most, most, ags.at[v.id], agr.at[v.id, 0], other).wait_send()
        cp = rcopy(part_of(v), part_of(v), dags.at[v.id], dagr.at[v.id], other)
        cp.wait_send()
        cp.wait_recv()

    rs_stages = [rs0, rs1] + [functools.partial(rsj, j) for j in range(TWO, PARTS + 1)] + [rs7, rs8, rs9]
    ag_stages = [ag1] + [functools.partial(agk, k) for k in range(TWO, PARTS + 2)] + [ag_end]

    def stage(fn, t, tables):
        for kind, table in zip((Full, Short), tables):
            w = NW
            for q, s in enumerate(table):
                w = jnp.where(t == s, q, w)

            @pl.when(w < NW)
            def _():
                fn(kind(w))

    def moves(t):
        for s in reversed(range(len(OFF))):
            stage(rs_stages[s], t - OFF[s], (START, SHORT_START))
        for q, fn in enumerate((dx1, dx2, dx3)):

            @pl.when((t == DX[0][q]) | (t == DX[1][q]))
            def _():
                fn(jnp.where(t == DX[1][q], 1, 0))

        for s in reversed(range(len(AGO))):
            stage(ag_stages[s], t - AGO[s], (AGS, SHORT_AGS))

    loads = [copy(x, acts.at[2], lsem.at[1]), copy(dy, acts.at[0], lsem.at[2])]
    rows_in = [copy(w.at[:, aligned(dp * OCT, OCT)], o, lsem.at[3 + k]) for k, (w, o) in enumerate(((w_gate, wr_g), (w_up, wr_u)))]
    rows_in.append(copy(w_down.at[:, aligned(div(OWN_ROWS * dp, OCT) * OCT, WIN, OCT)], wr_d, lsem.at[5]))
    moments = ((m_g, om_g), (m_u, om_u), (m_d, om_d), (v_g, ov_g), (v_u, ov_u), (v_d, ov_d))
    rows_in += [copy(m, o, lsem.at[6 + k]) for k, (m, o) in enumerate(moments)]
    for cp in loads + weights(0, 0, 0) + rows_in:
        cp.start()
    for q in range(OCT):
        da[pl.ds(q * CHIPS, CHIPS)] = jnp.zeros((CHIPS, ROWS, LANES), F32)
    loads[0].wait()
    by_rows(norm_in)
    transpose_in()
    a0t_out.start()
    for cp in rows_in:
        cp.wait()
    pl.semaphore_wait(barrier, GROUP - 1 + len(far))

    def tick(t, _):
        compute(t)
        moves(t)
        return 0

    lax.fori_loop(0, TICKS, tick, 0)


def step_call(args):
    B = (ROWS, LANES)
    V, R, S = pltpu.VMEM, pltpu.SemaphoreType.REGULAR, pltpu.SemaphoreType.DMA
    sizes = [TWO**k for k in reversed(range(PARTS))]
    n, ns = NW + NS, len(SHORT)
    own_parts = OWN_SLOTS * PARTS + NS * ns
    E = (PARTS, OCT, LANES)
    scratch = [
        V((3, TOK, D), BF), V((D, TOK), BF), V((4 * TB, *B), F32), V((4, D, TILE), BF), V((TWO, TILE, D), BF),
        *[V((TOK, TILE), BF)] * 3, V((TWO, TILE, TOK), BF), V((TWO, PAIR, TOK), BF), *[V((LAYERS, OCT, FF), BF)] * TWO, V((LAYERS, WIN, D), BF),
        V((TWO, own_parts, CHIPS, *B), BF), V((NDD, PARTS, CHIPS, *B), BF), V((NRS * PARTS * HALF, *B), F32),
        *[V((NRS, PARTS, k, *B), BF) for k in sizes * TWO],
        V((NS, ns, CHIPS, *B), BF), V((NS * ns * HALF, *B), F32),
        *[V((NS, ns, k, *B), BF) for k in sizes * TWO],
        V((NX + NS, TWO, *E), F32), V((n, *E), F32), V((NX + NS, TWO, *E), F32), V((n, *E), F32), V((n, PARTS, *B), BF),
        V((LAYERS, ROWS * (UNITS + 1), LANES), F32), *[V((LAYERS, GROUP, WIN, LANES), F32)] * 3,
        S((12,)), S((TWO, 3)), S((TWO,)), S((TWO, 2)), S((TWO,)), S((NDD + NS,)), S((NDD + NS,)), S((NRS + NS, PARTS)), S((NRS + NS, PARTS)),
        S((NX + NS,)), S((n,)), S((NX + NS,)), S((n,)), S((n,)), S((n,)), S((n, PARTS)), S((n,)), S((n,)), S((TWO, LAYERS)), S((TWO, LAYERS)),
        R((NDD,)), R((NRS,)),
    ]
    hbm, vmem = pl.BlockSpec(memory_space=pl.ANY), pl.BlockSpec(memory_space=pltpu.VMEM)
    out = [((NW, TWO, PARTS, CHIPS, *B), BF), ((NS, 2, ns, CHIPS, *B), BF), ((LAYERS, FF, TOK), BF), ((D, TOK), BF), ((TILES, TWO * TB, *B), F32)]
    out += [(s, F32) for s in ((LAYERS, OCT, FF), (LAYERS, OCT, FF), (LAYERS, WIN, D))] * TWO
    return pl.pallas_call(
        step_kernel,
        out_shape=[jax.ShapeDtypeStruct(*o) for o in out],
        in_specs=[hbm] * 11,
        out_specs=[hbm] * 5 + [vmem] * 6,
        scratch_shapes=scratch,
        compiler_params=pltpu.CompilerParams(collective_id=0, has_side_effects=True, vmem_limit_bytes=67043328),
        name="step",
    )(*args)


def place_kernel(
    ag, agm, om_g, om_u, om_d, ov_g, ov_u, ov_d, gate, up, down, pm_g, pm_u, pm_d, pv_g, pv_u, pv_d, buf, dbuf, mbuf, stage, mstage, dstage,
    isem, dsem, msem, osem, mosem, dosem,
):
    copy = pltpu.make_async_copy
    jobs = G0
    outs = (gate, up)

    def load(k):
        return copy(ag.at[jnp.where(k < D1, k, k + D1)], buf.at[mod(k, 2)], isem.at[mod(k, 2)])

    def stores(k):
        cols = aligned(LANES + PARTS * LANES * (mod(k, 4)), PARTS * LANES, LANES)
        return [copy(stage.at[mod(k, 2), m], o.at[jnp.where(k < D1, 1, 0), :, cols], osem.at[mod(k, 2), m]) for m, o in enumerate(outs)]

    def load_down(layer):
        return copy(ag.at[pl.ds(pick(layer, (D0, D1)), 2)], dbuf.at[layer], dsem.at[layer])

    def store_down(k):
        rows = aligned(mod(k, 4) * TWO * PAIR, TWO * PAIR, ROWS)
        return copy(dstage.at[mod(k, 2)], down.at[jnp.where(k < D1, 1, 0), rows], dosem.at[mod(k, 2)])

    def store_short(layer, m):
        return copy(mstage.at[layer, m], outs[m].at[layer, :, lanes(0)], mosem.at[layer, m])

    mini = copy(agm, mbuf, msem.at[0])
    for cp in (load_down(1), mini, load(0), load_down(0)):
        cp.start()
    for o, t in ((pm_g, om_g), (pm_u, om_u), (pv_g, ov_g), (pv_u, ov_u)):
        o[...] = t[...]
    for o, t in ((pm_d, om_d), (pv_d, ov_d)):
        o[...] = t[:, :OWN_ROWS]
    mini.wait()

    def by_chip(dst, cols, src, p):
        for u in range(CHIPS):
            n = CHIP_AT[u]
            dst[ROWS * n : ROWS * n + ROWS, cols] = src[rotl(u, p)]

    for layer in range(LAYERS):
        for m in range(TWO):
            by_chip(mstage.at[layer, m], lanes(0), mbuf.at[layer, m, 0], SHORT[0])
            store_short(layer, m).start()

    def body(k, _):
        layer = jnp.where(k < D1, 1, 0)

        @pl.when(mod(k, 4) == 0)
        def _():
            load_down(layer).wait()

        load(k).wait()

        @pl.when(k + 1 < jobs)
        def _():
            load(k + 1).start()

        @pl.when(k >= 2)
        def _():
            for cp in stores(k - 2) + [store_down(k - 2)]:
                cp.wait()

        for m in range(TWO):
            for p in range(PARTS):
                by_chip(stage.at[mod(k, 2), m], lanes(p), buf.at[mod(k, 2), m, p], p)
        for cp in stores(k):
            cp.start()

        def pair(q, _):
            for lt in range(OCT):
                h = lt // 4
                octets = []
                for gg in range(TWO):
                    g = (mod(k, 4) * TWO + q) * TWO + gg
                    spot = base_of(div(g, 4), mod(g, 4), 0) + base_of(0, 0, lt % 4)
                    for u in range(UNITS + 1):
                        if u < UNITS:
                            t = dbuf[layer, u // PARTS, h, u % PARTS, rotl(spot, u % PARTS)].astype(F32)
                        else:
                            t = mbuf[layer, h, 1, rotl(spot, SHORT[1])].astype(F32)[:OCT]
                        octets.append(t)
                dstage[mod(k, 2), aligned(PAIR * q, PAIR, ROWS), lanes(lt)] = jnp.concatenate(octets, 0).astype(BF)
            return 0

        lax.fori_loop(0, 2, pair, 0)
        store_down(k).start()
        return 0

    lax.fori_loop(0, jobs, body, 0)
    for k in (jobs - 2, jobs - 1):
        for cp in stores(k) + [store_down(k)]:
            cp.wait()
    for layer in range(LAYERS):
        for m in range(TWO):
            store_short(layer, m).wait()


def place_call(args):
    hbm, vmem = pl.BlockSpec(memory_space=pl.ANY), pl.BlockSpec(memory_space=pltpu.VMEM)
    V, S = pltpu.VMEM, pltpu.SemaphoreType.DMA
    whole = (TWO, PARTS, CHIPS, ROWS, LANES)
    out = [(s, BF) for s in ((LAYERS, D, FF), (LAYERS, D, FF), (LAYERS, FF, D))]
    out += [(s, F32) for s in ((LAYERS, OCT, FF), (LAYERS, OCT, FF), (LAYERS, OWN_ROWS, D))] * TWO
    return pl.pallas_call(
        place_kernel,
        out_shape=[jax.ShapeDtypeStruct(*o) for o in out],
        in_specs=[hbm] * TWO + [vmem] * 6,
        out_specs=[hbm] * 3 + [vmem] * 6,
        scratch_shapes=[
            V((TWO, *whole), BF), V((LAYERS, TWO, *whole), BF), V((NS, 2, len(SHORT), CHIPS, ROWS, LANES), BF),
            V((TWO, TWO, D, PARTS * LANES), BF), V((LAYERS, TWO, D, LANES), BF), V((TWO, TWO * PAIR, D), BF),
            S((TWO,)), S((TWO,)), S((1,)), S((TWO, 2)), S((TWO, 2)), S((TWO,)),
        ],
        compiler_params=pltpu.CompilerParams(vmem_limit_bytes=60 * TWO**20),
        name="place",
    )(*args)


def local_step(x, dy, w_gate, w_up, w_down, m_g, m_u, m_d, v_g, v_u, v_d):
    m_d, v_d = (jnp.pad(t, ((0, 0), (0, WIN - OWN_ROWS), (0, 0))) for t in (m_d, v_d))
    ag, agm, _, _, _, *moments = step_call((x[0], dy[0], w_gate, w_up, w_down, m_g, m_u, m_d, v_g, v_u, v_d))
    return tuple(place_call((ag, agm, *moments)))


def solution(mesh):
    moment = P(None, "dp", None)
    return jax.shard_map(
        local_step,
        mesh=mesh,
        in_specs=(P(("rep", "dp")), P(("rep", "dp")), P(), P(), P(), *[moment] * 6),
        out_specs=(P("rep"), P("rep"), P("rep"), *[P("rep", "dp", None)] * 6),
        check_vma=False,
    )
```

time: 1250 us -> 374 us (0.30); the launches traced: 1240 us -> 373 us
  blocking collectives: 664 us -> 0 us
  Pallas kernels: 0 us -> 366 us
  matrix products: 201 us -> 0 us
  starting transfers between devices: 155 us -> 0 us
  local copies, waits for them, and re-layouts: 104 us -> 7.02 us
  waiting for transfers between devices: 68.7 us -> 0 us
  other arithmetic: 27.7 us -> 0 us
  between operations: 14.9 us -> 0.66 us
    unnamed x2 -> x0, blocking collectives: 664 us -> none
    pallas_call x0 -> x2, Pallas kernels: none -> 366 us  [the longest x1 334 us: step_call(): pl.pallas_call(step_kernel, out_shape=[jax.ShapeDtypeStruct(*o) for o in...]
    dot_general x15 -> x0, matrix products: 201 us -> none  [the longest x5 71.3 us: layer(): up = jnp.dot(a, w['w_up'], preferred_element_type=jnp.float32)]
    unnamed x56 -> x0, starting transfers between devices: 155 us -> none
    unnamed x71 -> x2, local copies, waits for them, and re-layouts: 101 us -> 2 us
    reshape x3 -> x0, waiting for transfers between devices: 67.2 us -> none  [step(): t.reshape(-1, *t.shape[2:])]
    unnamed x8 -> x0, other arithmetic: 20.8 us -> none
  transfers between devices with their start and end apart: 59 -> 0, of which waited for: 2 -> 0; matrix products, arithmetic and copies ran while one was open for 39% -> 0% of each run, Pallas kernels for 0% -> 0%
where the time goes in v1:
time: 374 us; the launch traced here: 373 us
  Pallas kernels  366 us (98%)
  local copies, waits for them, and re-layouts  7.02 us (2%)
    pallas_call x1, Pallas kernels, step_call(): pl.pallas_call(step_kernel, out_shape=[jax.ShapeDtypeStruct(*o) for o in...  334 us
    pallas_call x1, Pallas kernels, place_call(): pl.pallas_call(place_kernel, out_shape=[jax.ShapeDtypeStruct(*o) for o in...  31.9 us

profile of v1, /device:TPU:1, one launch (start us, length us, event | category | flops | bytes accessed | tf_op | source)
XLA Modules:
  0.0 373.2 jit_solution(8330298297679042261)
XLA Ops:
  0.6 1.0 copy.20
  1.6 0.7 pad.7.m_d
  2.4 1.0 copy.21
  3.4 0.7 pad.8.v_d
  4.1 333.6 %step.1 = (bf16[12,2,6,64,16,128]{5,4,3,2,1,0:T(8,128)(2,1)}, bf16[2,2,2,64,16,128]{5,4,3,2,1,0:T(8,128)(2,1)}, bf16[2,3200,1024]{2,1,0:T(8,128)(2,1)}, bf16[102...) custom-call(bf16[1024,1024]{1,0:T(8,128)(2,1)} %bitcast.2, ...), custom_call_target="tpu_custom_call" | custom-call | tf_op jit(solution)/shard_map/step/pallas_call | solution.py:795
  337.7 31.9 %place.1 = (bf16[2,1024,3200]{2,1,0:T(8,128)(2,1)}, bf16[2,1024,3200]{2,1,0:T(8,128)(2,1)}, bf16[2,3200,1024]{2,1,0:T(8,128)(2,1)}, f32[2,8,3200]{2,1,0:T(8,128)...) custom-call(bf16[12,2,6,64,16,128]{5,4,3,2,1,0:T(8,128)(2,1)} %get-t, ...), custom_call_target="tpu_custom_call" | custom-call | tf_op jit(solution)/shard_map/place/pallas_call | solution.py:909
  369.6 1.8 copy.22
  371.4 1.8 copy.23

commit v2 on v1

--- a/solution.py
+++ b/solution.py
@@ -27,17 +27,17 @@
 NS = 2
 OWN_SLOT = (0, 1, 2, 0, 1, 2, 0, 3, 2, 0, 1, 2)
 OWN_SLOTS = 4
-NRS, NDD, NX = 4, 2, 4
+NRS, NDD, NX = 3, 2, 4
 
 T_F, T_FN, T_L1, T_DOWN1, T_NORM, T_DOWN0, T_B0, T_TAIL = 0, 13, 14, 40, 44, 45, 49, 62
-START = (21, 27, 33, 39, 43, 44, 48, 49, 52, 55, 58, 61)
+START = (21, 27, 33, 39, 43, 45, 49, 51, 53, 57, 59, 61)
 SHORT_START = (50, 45)
 OFF = (0, 2, 4, 6, 7, 8, 9, 10, 11, 12)
-DX = ((61, 63, 65), (56, 58, 60))
-AGS = (33, 39, 45, 51, 60, 61, 65, 66, 64, 67, 70, 73)
-SHORT_AGS = (65, 60)
+DX = ((62, 64, 66), (56, 58, 60))
+AGS = (33, 39, 45, 51, 61, 63, 67, 69, 65, 71, 73, 75)
+SHORT_AGS = (67, 61)
 AGO = (0, 2, 4, 6, 8, 10, 13, 16)
-TICKS = 90
+TICKS = 92
 
 
 def div(a, b):
@@ -46,6 +46,10 @@
 
 def mod(a, b):
     return a % b if isinstance(a, int) else lax.rem(a, jnp.int32(b))
+
+
+def loop(n, fn):
+    lax.fori_loop(0, n, fn, 0)
 
 
 def base_of(x, y, z):
@@ -112,7 +116,7 @@
 def step_kernel(
     x, dy, w_gate, w_up, w_down, m_g, m_u, m_d, v_g, v_u, v_d,
     ag, agm, hidt, a0t, gu0, om_g, om_u, om_d, ov_g, ov_u, ov_d,
-    acts, at, da, wgu, wdb, dgb, dub, hidb, hts, htb, wr_g, wr_u, wr_d,
+    acts, at, da, wgu, wdb, dgu, hidb, hts, htb, wr_g, wr_u, wr_d, md, vd,
     own, d2d, acc, r1, r2, r3, r4, r5, r6, s1, s2, s3, s4, s5, s6,
     d2dm, accm, q1, q2, q3, q4, q5, q6, t1, t2, t3, t4, t5, t6,
     gfin, xg, wsend, wrecv, fin, g_d, gx, ws_d, wx,
@@ -158,7 +162,7 @@
         down = [copy(w_down.at[layer, o], wdb.at[b], wsem.at[b, 2])]
         if not gate_up:
             return down
-        return down + [copy(w.at[layer, :, o], wgu.at[TWO * b + k], wsem.at[b, k]) for k, w in enumerate((w_gate, w_up))]
+        return down + [copy(w.at[layer, :, o], wgu.at[b, :, pl.ds(TILE * k, TILE)], wsem.at[b, k]) for k, w in enumerate((w_gate, w_up))]
 
     def saved(i, b):
         return weights(0, i, b, False) + [copy(gu0.at[i], da.at[pl.ds(b * TWO * TB, TWO * TB)], gsem.at[b])]
@@ -172,18 +176,12 @@
             for cp in make(i + 1, 1 - b):
                 cp.start()
 
-    def halves(fn):
-        def chunk(k, _):
-            fn(k, aligned(k * (TOK // TWO), TOK // TWO))
-            return 0
-
-        lax.fori_loop(0, 2, chunk, 0)
-
     def as_blocks(v):
         return v.reshape(v.shape[0] // ROWS, ROWS, LANES)
 
     def get_da(q, rows, n):
-        return da[pl.ds(q * CHIPS + div(rows, ROWS), n // ROWS)].reshape(n, LANES)
+        at_row = rows // ROWS if isinstance(rows, int) else div(rows, ROWS)
+        return da[pl.ds(q * CHIPS + at_row, n // ROWS)].reshape(n, LANES)
 
     def sigmoid(v):
         return 1.0 / (1.0 + jnp.exp(-v))
@@ -194,17 +192,12 @@
         return s, dhid * up * (sg * (1.0 + gate * (1.0 - sg))), dhid * s
 
     def counts(i):
-        return (lax.broadcasted_iota(jnp.int32, (TOK // TWO, TILE), 1) < LANES) | (i > 0)
-
-    def add_products(terms):
-        def part(n, _):
-            total = sum(dot(a[...], *rhs(n)) for a, rhs in terms)
-            for q in range(TWO):
-                o = pl.ds((TWO * n + q) * CHIPS, CHIPS)
-                da[o] = da[o] + as_blocks(total[:, lanes(q)])
-            return 0
-
-        lax.fori_loop(0, D // TILE, part, 0)
+        return (lax.broadcasted_iota(jnp.int32, (TOK, TILE), 1) < LANES) | (i > 0)
+
+    def add_product(t):
+        for q in range(OCT):
+            o = pl.ds(q * CHIPS, CHIPS)
+            da[o] = da[o] + as_blocks(t[:, lanes(q)])
 
     def hid_write(layer, i, b, q):
         o = pl.multiple_of(off_of(i) + LANES * q, LANES)
@@ -240,17 +233,13 @@
         def _():
             gu_out(i - 2, b).wait()
 
-        def chunk(k, rows):
-            gate = dot(acts[1, rows], wgu[TWO * b])
-            up = dot(acts[1, rows], wgu[TWO * b + 1])
-            hidb[rows] = jnp.where(counts(i), gate * sigmoid(gate) * up, 0.0).astype(BF)
-            for m, t in enumerate((gate, up)):
-                for q in range(TWO):
-                    acc[pl.ds((TWO * b + m) * TB + q * CHIPS + k * HALF, HALF)] = as_blocks(t[:, lanes(q)])
-
-        halves(chunk)
+        gu = dot(acts[1], wgu[b])
+        gate, up = gu[:, :TILE], gu[:, TILE:]
+        hidb[...] = jnp.where(counts(i), gate * sigmoid(gate) * up, 0.0).astype(BF)
+        for q in range(4):
+            acc[pl.ds(TWO * b * TB + q * CHIPS, CHIPS)] = as_blocks(gu[:, lanes(q)])
         gu_out(i, b).start()
-        add_products([(hidb, lambda n: (wdb[b, :, aligned(n * TILE, TILE)],))])
+        add_product(dot(hidb[...], wdb[b]))
         put_hidden(0, i, b)
 
     def transpose_in():
@@ -261,14 +250,14 @@
                 at[aligned(base_of(div(n, 16), mod(div(n, 4), 4), mod(n, 4)) * ROWS, ROWS)] = t[q * ROWS : (q + 1) * ROWS]
             return 0
 
-        lax.fori_loop(0, D // LANES, part, 0)
+        loop(D // LANES, part)
 
     def by_rows(fn):
         def chunk(k, _):
             fn(k * LANES, aligned(k * LANES, LANES))
             return 0
 
-        lax.fori_loop(0, TOK // LANES, chunk, 0)
+        loop(TOK // LANES, chunk)
 
     def norm_in(_, rows):
         h = acts[2, rows].astype(F32)
@@ -294,32 +283,22 @@
         b = mod(i, 2)
         stream(functools.partial(weights, 1), i, b)
 
-        def chunk(_, rows):
-            gate = dot(acts[1, rows], wgu[TWO * b])
-            up = dot(acts[1, rows], wgu[TWO * b + 1])
-            dhid = dot(acts[0, rows], wdb[b], 1).astype(BF).astype(F32)
-            s, dgate, dup = through_act(gate, up, dhid)
-            hidb[rows] = (s * up).astype(BF)
-            dgb[rows] = jnp.where(counts(i), dgate, 0.0).astype(BF)
-            dub[rows] = jnp.where(counts(i), dup, 0.0).astype(BF)
-
-        halves(chunk)
+        gu = dot(acts[1], wgu[b])
+        gate, up = gu[:, :TILE], gu[:, TILE:]
+        dhid = dot(acts[0], wdb[b], 1).astype(BF).astype(F32)
+        s, dgate, dup = through_act(gate, up, dhid)
+        hidb[...] = (s * up).astype(BF)
+        dgu[:, :TILE] = jnp.where(counts(i), dgate, 0.0).astype(BF)
+        dgu[:, TILE:] = jnp.where(counts(i), dup, 0.0).astype(BF)
 
     def grads_gate_up(i, slot, layer):
         first = i == 0
         part = slot * PARTS + TWO * mod(i + 2, 3)
         pa = jnp.where(first, OWN_SLOTS * PARTS + TWO * layer, part)
         pb = jnp.where(first, slot * PARTS, part + 1)
-
-        def chunk(k, rows):
-            blocks = pl.ds(k * HALF, HALF)
-            lhs = at[rows]
-            for mat, src in enumerate((dgb, dub)):
-                r = dot(lhs, src[...]).astype(BF)
-                for q, p in enumerate((pa, pb)):
-                    own[mat, p, blocks] = as_blocks(r[:, lanes(q)])
-
-        halves(chunk)
+        r = dot(at[...], dgu[...]).astype(BF)
+        for q in range(4):
+            own[q // TWO, pb if q % TWO else pa] = as_blocks(r[:, lanes(q)])
 
     def wave_in_layer(i):
         return div(jnp.maximum(i - 1, 0), 3)
@@ -327,7 +306,7 @@
     def tick_b(i):
         b = mod(i, 2)
         grads_gate_up(i, mod(wave_in_layer(i), 3), 1)
-        add_products([(t, lambda n, m=m: (wgu[TWO * b + m, aligned(n * TILE, TILE)], 1)) for m, t in enumerate((dgb, dub))])
+        add_product(dot(dgu[...], wgu[b], 1))
         put_hidden(1, i, b)
 
     def hid_load(layer, r):
@@ -372,16 +351,11 @@
         b = mod(i, 2)
         stream(saved, i, b)
 
-        def chunk(k, rows):
-            dhid = dot(acts[1, rows], wdb[b], 1).astype(BF).astype(F32)
-            gate, up = (
-                jnp.concatenate([get_da(4 * b + TWO * m + q, k * (TOK // TWO), TOK // TWO) for q in range(TWO)], 1) for m in range(TWO)
-            )
-            _, dgate, dup = through_act(gate, up, dhid)
-            dgb[rows] = dgate.astype(BF)
-            dub[rows] = dup.astype(BF)
-
-        halves(chunk)
+        dhid = dot(acts[1], wdb[b], 1).astype(BF).astype(F32)
+        gate, up = (jnp.concatenate([get_da(4 * b + TWO * m + q, 0, TOK) for q in range(TWO)], 1) for m in range(TWO))
+        _, dgate, dup = through_act(gate, up, dhid)
+        dgu[:, :TILE] = dgate.astype(BF)
+        dgu[:, TILE:] = dup.astype(BF)
         grads_gate_up(i, pick(wave_in_layer(i), OWN_SLOT[G0:]), 0)
 
     a0t_out = copy(at, a0t, lsem.at[0])
@@ -516,7 +490,7 @@
                     v.accumulated[acc_at(v, k) + g * OCT + i] = both[1]
                 return 0
 
-            lax.fori_loop(0, HALF // OCT, some, 0)
+            loop(HALF // OCT, some)
             return stage_one(v, 1, k)
 
         lag_start([functools.partial(make, k) for k in range(len(v.parts))])
@@ -648,6 +622,13 @@
             return g_d.at[layer, aligned(window(j), WIN, OCT)]
 
         to_group(0, layer, src, gx)
+
+        def row(r, _):
+            for o, t in ((om_d, md), (ov_d, vd)):
+                o[layer, pl.ds(r, 1)] = t[r, pl.ds(layer, 1)]
+            return 0
+
+        loop(OWN_ROWS, row)
         gx[layer, j_me] = g_d[layer, aligned(window(j_me), WIN, OCT)]
 
     def dx2(layer):
@@ -664,7 +645,7 @@
             ws_d[layer, lt] = jnp.where(valid, wn, 0.0)
             return 0
 
-        lax.fori_loop(0, OCT, tile, 0)
+        loop(OCT, tile)
 
         def src(j):
             return ws_d.at[layer, 4 * mod(j, 2) + div(j, 2)]
@@ -722,32 +703,49 @@
     rs_stages = [rs0, rs1] + [functools.partial(rsj, j) for j in range(TWO, PARTS + 1)] + [rs7, rs8, rs9]
     ag_stages = [ag1] + [functools.partial(agk, k) for k in range(TWO, PARTS + 2)] + [ag_end]
 
-    def stage(fn, t, tables):
-        for kind, table in zip((Full, Short), tables):
-            w = NW
-            for q, s in enumerate(table):
-                w = jnp.where(t == s, q, w)
-
-            @pl.when(w < NW)
-            def _():
-                fn(kind(w))
+    def find(t, table):
+        terms = [jnp.where(t == s, q + 1, 0) for q, s in enumerate(table)]
+        while len(terms) > 1:
+            terms = [sum(terms[q : q + 2]) for q in range(0, len(terms), 2)]
+        return terms[0]
+
+    def run(fns, offs, s, t, kind, table):
+        w = find(t - offs[s], table)
+
+        @pl.when(w > 0)
+        def _():
+            fns[s](kind(w - 1))
+
+    def stages(fns, offs, t, table, short_table):
+        @pl.when((t >= min(table)) & (t <= max(table) + offs[-1]))
+        def _():
+            for odd in range(TWO):
+
+                @pl.when(mod(t, 2) == odd)
+                def _():
+                    for s in reversed(range(len(offs))):
+                        if (offs[s] + 1) % TWO == odd:
+                            run(fns, offs, s, t, Full, table)
+
+        @pl.when((t >= min(short_table)) & (t <= max(short_table) + offs[-1]))
+        def _():
+            for s in reversed(range(len(offs))):
+                run(fns, offs, s, t, Short, short_table)
 
     def moves(t):
-        for s in reversed(range(len(OFF))):
-            stage(rs_stages[s], t - OFF[s], (START, SHORT_START))
+        stages(rs_stages, OFF, t, START, SHORT_START)
         for q, fn in enumerate((dx1, dx2, dx3)):
 
             @pl.when((t == DX[0][q]) | (t == DX[1][q]))
             def _():
                 fn(jnp.where(t == DX[1][q], 1, 0))
 
-        for s in reversed(range(len(AGO))):
-            stage(ag_stages[s], t - AGO[s], (AGS, SHORT_AGS))
+        stages(ag_stages, AGO, t, AGS, SHORT_AGS)
 
     loads = [copy(x, acts.at[2], lsem.at[1]), copy(dy, acts.at[0], lsem.at[2])]
     rows_in = [copy(w.at[:, aligned(dp * OCT, OCT)], o, lsem.at[3 + k]) for k, (w, o) in enumerate(((w_gate, wr_g), (w_up, wr_u)))]
     rows_in.append(copy(w_down.at[:, aligned(div(OWN_ROWS * dp, OCT) * OCT, WIN, OCT)], wr_d, lsem.at[5]))
-    moments = ((m_g, om_g), (m_u, om_u), (m_d, om_d), (v_g, ov_g), (v_u, ov_u), (v_d, ov_d))
+    moments = ((m_g, om_g), (m_u, om_u), (m_d, md), (v_g, ov_g), (v_u, ov_u), (v_d, vd))
     rows_in += [copy(m, o, lsem.at[6 + k]) for k, (m, o) in enumerate(moments)]
     for cp in loads + weights(0, 0, 0) + rows_in:
         cp.start()
@@ -766,7 +764,7 @@
         moves(t)
         return 0
 
-    lax.fori_loop(0, TICKS, tick, 0)
+    loop(TICKS, tick)
 
 
 def step_call(args):
@@ -777,8 +775,9 @@
     own_parts = OWN_SLOTS * PARTS + NS * ns
     E = (PARTS, OCT, LANES)
     scratch = [
-        V((3, TOK, D), BF), V((D, TOK), BF), V((4 * TB, *B), F32), V((4, D, TILE), BF), V((TWO, TILE, D), BF),
-        *[V((TOK, TILE), BF)] * 3, V((TWO, TILE, TOK), BF), V((TWO, PAIR, TOK), BF), *[V((LAYERS, OCT, FF), BF)] * TWO, V((LAYERS, WIN, D), BF),
+        V((3, TOK, D), BF), V((D, TOK), BF), V((4 * TB, *B), F32), V((TWO, D, TWO * TILE), BF), V((TWO, TILE, D), BF),
+        V((TOK, TWO * TILE), BF), V((TOK, TILE), BF), V((TWO, TILE, TOK), BF), V((TWO, PAIR, TOK), BF),
+        *[V((LAYERS, OCT, FF), BF)] * TWO, V((LAYERS, WIN, D), BF), *[V((OWN_ROWS, LAYERS, D), F32)] * TWO,
         V((TWO, own_parts, CHIPS, *B), BF), V((NDD, PARTS, CHIPS, *B), BF), V((NRS * PARTS * HALF, *B), F32),
         *[V((NRS, PARTS, k, *B), BF) for k in sizes * TWO],
         V((NS, ns, CHIPS, *B), BF), V((NS * ns * HALF, *B), F32),
@@ -834,7 +833,9 @@
     for o, t in ((pm_g, om_g), (pm_u, om_u), (pv_g, ov_g), (pv_u, ov_u)):
         o[...] = t[...]
     for o, t in ((pm_d, om_d), (pv_d, ov_d)):
-        o[...] = t[:, :OWN_ROWS]
+        for layer in range(LAYERS):
+            for r in range(OWN_ROWS):
+                o[r, layer : layer + 1] = t[layer, r : r + 1]
     mini.wait()
 
     def by_chip(dst, cols, src, p):
@@ -887,11 +888,11 @@
                 dstage[mod(k, 2), aligned(PAIR * q, PAIR, ROWS), lanes(lt)] = jnp.concatenate(octets, 0).astype(BF)
             return 0
 
-        lax.fori_loop(0, 2, pair, 0)
+        loop(2, pair)
         store_down(k).start()
         return 0
 
-    lax.fori_loop(0, jobs, body, 0)
+    loop(jobs, body)
     for k in (jobs - 2, jobs - 1):
         for cp in stores(k) + [store_down(k)]:
             cp.wait()
@@ -905,7 +906,7 @@
     V, S = pltpu.VMEM, pltpu.SemaphoreType.DMA
     whole = (TWO, PARTS, CHIPS, ROWS, LANES)
     out = [(s, BF) for s in ((LAYERS, D, FF), (LAYERS, D, FF), (LAYERS, FF, D))]
-    out += [(s, F32) for s in ((LAYERS, OCT, FF), (LAYERS, OCT, FF), (LAYERS, OWN_ROWS, D))] * TWO
+    out += [(s, F32) for s in ((LAYERS, OCT, FF), (LAYERS, OCT, FF), (OWN_ROWS, LAYERS, D))] * TWO
     return pl.pallas_call(
         place_kernel,
         out_shape=[jax.ShapeDtypeStruct(*o) for o in out],
@@ -922,9 +923,11 @@
 
 
 def local_step(x, dy, w_gate, w_up, w_down, m_g, m_u, m_d, v_g, v_u, v_d):
-    m_d, v_d = (jnp.pad(t, ((0, 0), (0, WIN - OWN_ROWS), (0, 0))) for t in (m_d, v_d))
+    m_d, v_d = (jnp.transpose(t, (1, 0, 2)) for t in (m_d, v_d))
     ag, agm, _, _, _, *moments = step_call((x[0], dy[0], w_gate, w_up, w_down, m_g, m_u, m_d, v_g, v_u, v_d))
-    return tuple(place_call((ag, agm, *moments)))
+    gate, up, down, om_g, om_u, om_d, ov_g, ov_u, ov_d = place_call((ag, agm, *moments))
+    om_d, ov_d = (jnp.transpose(t, (1, 0, 2)) for t in (om_d, ov_d))
+    return gate, up, down, om_g, om_u, om_d, ov_g, ov_u, ov_d
 
 
 def solution(mesh):

time: 374 us -> 338 us (0.904)
  Pallas kernels: 366 us -> 336 us
  local copies, waits for them, and re-layouts: 7.02 us -> 0 us
    pallas_call x1, Pallas kernels: 334 us -> 305 us  [step_call(): pl.pallas_call(step_kernel, out_shape=[jax.ShapeDtypeStruct(*o) for o in...]
where the time goes in v2:
time: 338 us; the launch traced here: 337 us
  Pallas kernels  336 us (99%)
    pallas_call x1, Pallas kernels, step_call(): pl.pallas_call(step_kernel, out_shape=[jax.ShapeDtypeStruct(*o) for o in...  305 us
    pallas_call x1, Pallas kernels, place_call(): pl.pallas_call(place_kernel, out_shape=[jax.ShapeDtypeStruct(*o) for o in...  31.8 us

profile of v2, /device:TPU:1, one launch (start us, length us, event | category | flops | bytes accessed | tf_op | source)
XLA Modules:
  0.0 337.1 jit_solution(17197965481042080255)
XLA Ops:
  0.6 304.6 %step.1 = (bf16[12,2,6,64,16,128]{5,4,3,2,1,0:T(8,128)(2,1)}, bf16[2,2,2,64,16,128]{5,4,3,2,1,0:T(8,128)(2,1)}, bf16[2,3200,1024]{2,1,0:T(8,128)(2,1)}, bf16[102...) custom-call(bf16[1024,1024]{1,0:T(8,128)(2,1)} %bitcast.6, ...), custom_call_target="tpu_custom_call" | custom-call | tf_op jit(solution)/shard_map/step/pallas_call | solution.py:794
  305.2 31.8 %place.1 = (bf16[2,1024,3200]{2,1,0:T(8,128)(2,1)}, bf16[2,1024,3200]{2,1,0:T(8,128)(2,1)}, bf16[2,3200,1024]{2,1,0:T(8,128)(2,1)}, f32[2,8,3200]{2,1,0:T(8,128)...) custom-call(bf16[12,2,6,64,16,128]{5,4,3,2,1,0:T(8,128)(2,1)} %get-t, ...), custom_call_target="tpu_custom_call" | custom-call | tf_op jit(solution)/shard_map/place/pallas_call | solution.py:910

commit v3 on v2

--- a/solution.py
+++ b/solution.py
@@ -1,4 +1,5 @@
 import functools
+from itertools import accumulate
 
 import jax
 import jax.numpy as jnp
@@ -8,7 +9,7 @@
 from jax.sharding import PartitionSpec as P
 
 MESH = pl.DeviceIdType.MESH
-TWO = 2
+ONE, TWO = 1, 2
 BF, F32 = jnp.bfloat16, jnp.float32
 LAYERS, D, FF, TOK = 2, 1024, 3200, 1024
 LANES, ROWS, OCT = 128, 16, 8
@@ -21,6 +22,8 @@
 UNITS = ROWS_GROUP // ROWS
 OWN_ROWS = ROWS_GROUP // GROUP
 WIN = 32
+RUN = 16
+DEEP = 3
 
 G1, D1, D0, G0, NW = 0, 4, 6, 8, 12
 SHORT = (0, 3)
@@ -29,15 +32,19 @@
 OWN_SLOTS = 4
 NRS, NDD, NX = 3, 2, 4
 
-T_F, T_FN, T_L1, T_DOWN1, T_NORM, T_DOWN0, T_B0, T_TAIL = 0, 13, 14, 40, 44, 45, 49, 62
-START = (21, 27, 33, 39, 43, 45, 49, 51, 53, 57, 59, 61)
-SHORT_START = (50, 45)
-OFF = (0, 2, 4, 6, 7, 8, 9, 10, 11, 12)
-DX = ((62, 64, 66), (56, 58, 60))
-AGS = (33, 39, 45, 51, 61, 63, 67, 69, 65, 71, 73, 75)
-SHORT_AGS = (67, 61)
-AGO = (0, 2, 4, 6, 8, 10, 13, 16)
-TICKS = 92
+T_F, T_FN, T_L1, T_DOWN1, T_DA, T_NORM, T_DOWN0, T_B0, T_TAIL = 0, 13, 14, 40, 44, 51, 52, 56, 69
+
+
+def ticks(codes):
+    return tuple(tuple(accumulate((ord(ch) - ord("0") for ch in code), initial=20))[1:] for code in codes)
+
+
+RS_TICKS = ticks(('34427211', '74623257', '=4421211', 'C4223211', 'G2241417', 'K422521=', 'S2221271', 'U422143;', 'W4223433', '[2243473', ']6421831', 'a6263411'))
+SHORT_RS_TICKS = ticks(('T2221693', 'I1242751'))
+AG_TICKS = ticks(('J34;>A', 'Z96SP7', 'L343TE', 'T56=DM', '^A49>7', '`7:3JA', 'h;D9:C', 'p9:A@A', 'l;8?:3', 't9F?85', 'vC6I:9', 'x=L5:9'))
+SHORT_AG_TICKS = ticks(('q6@@G9', 't=E>;;'))
+DX = ticks(('e12', 'Z12'))
+TICKS = max(max(t) for t in AG_TICKS + SHORT_AG_TICKS) + 1
 
 
 def div(a, b):
@@ -78,6 +85,11 @@
     return rotl(u, (PARTS - p) % PARTS)
 
 
+def _flips(p):
+    dims = [ORDER[(p + j) % PARTS] for j in (3, 4, 5)]
+    return [tuple(d for d, bit in zip(dims, (4, 2, 1)) if e & bit) for e in range(1, OCT)]
+
+
 def off_of(i):
     return pl.multiple_of(jnp.maximum(TILE * i - LANES, 0), LANES)
 
@@ -115,12 +127,12 @@
 
 def step_kernel(
     x, dy, w_gate, w_up, w_down, m_g, m_u, m_d, v_g, v_u, v_d,
-    ag, agm, hidt, a0t, gu0, om_g, om_u, om_d, ov_g, ov_u, ov_d,
+    ag, agm, hidt, a0t, gu0, dgh, om_g, om_u, om_d, ov_g, ov_u, ov_d,
     acts, at, da, wgu, wdb, dgu, hidb, hts, htb, wr_g, wr_u, wr_d, md, vd,
-    own, d2d, acc, r1, r2, r3, r4, r5, r6, s1, s2, s3, s4, s5, s6,
-    d2dm, accm, q1, q2, q3, q4, q5, q6, t1, t2, t3, t4, t5, t6,
+    own, d2d, acc, r1, r2, r3, r4, s1, s2, s3, s4,
+    d2dm, accm, q1, q2, q3, q4, t1, t2, t3, t4,
     gfin, xg, wsend, wrecv, fin, g_d, gx, ws_d, wx,
-    lsem, wsem, gsem, hsem, htsem, d2s, d2r, ssem, rsem, xs, xr, wsm, wrm, agl, ags, agr, dags, dagr, dxs, dxr, d2c, rcred,
+    lsem, wsem, gsem, dsem, hsem, htsem, d2s, d2r, ssem, rsem, xs, xr, wsm, wrm, agl, ags, agr, dags, dagr, dxs, dxr, d2c, rcred,
 ):
     dp = lax.axis_index("dp")
     c = mod(dp, 2)
@@ -131,12 +143,17 @@
     def device(x, y, z, core):
         return ((x * 4 + y) * 4 + z) * TWO + core
 
-    def partner(d):
-        o = pos[d[0]]
-        return device(**(pos | {d[0]: 3 - o if d.endswith("1") else o + 1 - TWO * mod(o, 2)}), core=c)
+    def flipped(*dims):
+        at = dict(pos)
+        for d in dims:
+            o = pos[d[0]]
+            at[d[0]] = 3 - o if d.endswith("1") else o + 1 - TWO * mod(o, 2)
+        return device(**at, core=c)
 
     bits = [gray(pos[d[0]], d) for d in ORDER]
-    partners = [partner(d) for d in ORDER]
+    partners = [flipped(d) for d in ORDER]
+    near = [_flips(p) for p in range(PARTS)]
+    across = {dims: flipped(*dims) for dims in dict.fromkeys(d for ds in near for d in ds)}
     rot = [rotl(base_of(**pos), p) for p in range(PARTS)]
 
     def group_dev(j):
@@ -153,16 +170,16 @@
     barrier = pltpu.get_barrier_semaphore()
     for r in range(1, GROUP):
         signal(barrier, group_dev(mod(j_me + r, GROUP)))
-    far = [q for d, q in zip(ORDER, partners) if d[0] != "z"]
+    far = [q for dims, q in across.items() if dims not in (("z1",), ("z0",))]
     for q in far:
         signal(barrier, q)
 
-    def weights(layer, i, b, gate_up=True):
+    def weights(layer, i, b, gate_up=True, down=True):
         o = pl.ds(off_of(i), TILE)
-        down = [copy(w_down.at[layer, o], wdb.at[b], wsem.at[b, 2])]
+        some = [copy(w_down.at[layer, o], wdb.at[b], wsem.at[b, 2])] if down else []
         if not gate_up:
-            return down
-        return down + [copy(w.at[layer, :, o], wgu.at[b, :, pl.ds(TILE * k, TILE)], wsem.at[b, k]) for k, w in enumerate((w_gate, w_up))]
+            return some
+        return some + [copy(w.at[layer, :, o], wgu.at[b, :, pl.ds(TILE * k, TILE)], wsem.at[b, k]) for k, w in enumerate((w_gate, w_up))]
 
     def saved(i, b):
         return weights(0, i, b, False) + [copy(gu0.at[i], da.at[pl.ds(b * TWO * TB, TWO * TB)], gsem.at[b])]
@@ -173,7 +190,7 @@
 
         @pl.when(i + 1 < TILES)
         def _():
-            for cp in make(i + 1, 1 - b):
+            for cp in make(i + 1, ONE - b):
                 cp.start()
 
     def as_blocks(v):
@@ -279,35 +296,64 @@
         transpose_in()
         hidden_out(0)
 
+    def dgu_out(i, b):
+        return copy(dgu.at[b], dgh.at[i], dsem.at[b])
+
     def tick_a(i):
         b = mod(i, 2)
         stream(functools.partial(weights, 1), i, b)
+
+        @pl.when(i >= 2)
+        def _():
+            dgu_out(i - 2, b).wait()
+
 
         gu = dot(acts[1], wgu[b])
         gate, up = gu[:, :TILE], gu[:, TILE:]
         dhid = dot(acts[0], wdb[b], 1).astype(BF).astype(F32)
         s, dgate, dup = through_act(gate, up, dhid)
         hidb[...] = (s * up).astype(BF)
-        dgu[:, :TILE] = jnp.where(counts(i), dgate, 0.0).astype(BF)
-        dgu[:, TILE:] = jnp.where(counts(i), dup, 0.0).astype(BF)
-
-    def grads_gate_up(i, slot, layer):
+        dgu[b, :, :TILE] = jnp.where(counts(i), dgate, 0.0).astype(BF)
+        dgu[b, :, TILE:] = jnp.where(counts(i), dup, 0.0).astype(BF)
+
+    def grads_gate_up(i, slot, layer, cuts):
         first = i == 0
         part = slot * PARTS + TWO * mod(i + 2, 3)
         pa = jnp.where(first, OWN_SLOTS * PARTS + TWO * layer, part)
         pb = jnp.where(first, slot * PARTS, part + 1)
-        r = dot(at[...], dgu[...]).astype(BF)
-        for q in range(4):
-            own[q // TWO, pb if q % TWO else pa] = as_blocks(r[:, lanes(q)])
+        n = D // cuts
+
+        def chunk(k, _):
+            r = dot(at[aligned(k * n, n)], dgu[mod(i, 2)]).astype(BF)
+            for q in range(4):
+                own[q // TWO, pb if q % TWO else pa, pl.ds(k * (n // ROWS), n // ROWS)] = as_blocks(r[:, lanes(q)])
+            return 0
+
+        if cuts == 1:
+            chunk(0, 0)
+        else:
+            loop(cuts, chunk)
 
     def wave_in_layer(i):
         return div(jnp.maximum(i - 1, 0), 3)
 
     def tick_b(i):
         b = mod(i, 2)
-        grads_gate_up(i, mod(wave_in_layer(i), 3), 1)
-        add_product(dot(dgu[...], wgu[b], 1))
+        grads_gate_up(i, mod(wave_in_layer(i), 3), 1, 1)
+        dgu_out(i, b).start()
         put_hidden(1, i, b)
+
+    def da_loads(i, b):
+        return weights(1, i, b, down=False) + [copy(dgh.at[i], dgu.at[b], dsem.at[b])]
+
+    def tick_da(k):
+        def iteration(i, _):
+            b = mod(i, 2)
+            stream(da_loads, i, b)
+            add_product(dot(dgu[b], wgu[b], 1))
+            return 0
+
+        lax.fori_loop(TWO * k, jnp.minimum(TWO * k + 2, TILES), iteration, 0)
 
     def hid_load(layer, r):
         return copy(hidt.at[layer, aligned(PAIR * r, PAIR, ROWS)], htb.at[mod(r, 2)], htsem.at[mod(r, 2)])
@@ -321,7 +367,7 @@
                 hid_load(layer, r + 1).start()
 
             slots = [jnp.where(layer == 1, OWN_SLOT[D1 + q], OWN_SLOT[D0 + q]) * PARTS for q in range(TWO)]
-            res = dot(htb[mod(r, 2)], acts[1 - layer])
+            res = dot(htb[mod(r, 2)], acts[ONE - layer])
             for gg in range(TWO):
                 g = TWO * r + gg
                 at_xy = base_of(div(g, 4), mod(g, 4), 0)
@@ -351,12 +397,18 @@
         b = mod(i, 2)
         stream(saved, i, b)
 
-        dhid = dot(acts[1], wdb[b], 1).astype(BF).astype(F32)
-        gate, up = (jnp.concatenate([get_da(4 * b + TWO * m + q, 0, TOK) for q in range(TWO)], 1) for m in range(TWO))
-        _, dgate, dup = through_act(gate, up, dhid)
-        dgu[:, :TILE] = dgate.astype(BF)
-        dgu[:, TILE:] = dup.astype(BF)
-        grads_gate_up(i, pick(wave_in_layer(i), OWN_SLOT[G0:]), 0)
+        def chunk(k, _):
+            n = TOK // TWO
+            rows = aligned(k * n, n)
+            dhid = dot(acts[1, rows], wdb[b], 1).astype(BF).astype(F32)
+            gate, up = (jnp.concatenate([get_da(4 * b + TWO * m + q, k * n, n) for q in range(TWO)], 1) for m in range(TWO))
+            _, dgate, dup = through_act(gate, up, dhid)
+            dgu[b, rows, :TILE] = dgate.astype(BF)
+            dgu[b, rows, TILE:] = dup.astype(BF)
+            return 0
+
+        loop(2, chunk)
+        grads_gate_up(i, pick(wave_in_layer(i), OWN_SLOT[G0:]), 0, 2)
 
     a0t_out = copy(at, a0t, lsem.at[0])
     a0t_in = copy(a0t, at, lsem.at[0])
@@ -392,11 +444,17 @@
         @pl.when(t == T_DOWN1)
         def _():
             hidden_out(1)
-
-        @pl.when(((t >= T_DOWN1) & (t < T_NORM)) | ((t >= T_DOWN0) & (t < T_B0)))
+            for i in (TILES - 2, TILES - 1):
+                dgu_out(i, i % TWO).wait()
+            for cp in da_loads(0, 0):
+                cp.start()
+
+        @pl.when(((t >= T_DOWN1) & (t < T_DA)) | ((t >= T_DOWN0) & (t < T_B0)))
         def _():
             layer = jnp.where(t < T_NORM, 1, 0)
             tick_down(t - jnp.where(t < T_NORM, T_DOWN1, T_DOWN0), layer)
+
+        between(T_DA, T_NORM, tick_da)
 
         @pl.when(t == T_NORM)
         def _():
@@ -427,7 +485,7 @@
 
     class Full:
         parts = tuple(range(PARTS))
-        accumulated, received, sent, crossed, ag_ref = acc, (None, r1, r2, r3, r4, r5, r6), (None, s1, s2, s3, s4, s5, s6), d2d, ag
+        accumulated, received, sent, crossed, ag_ref = acc, (None, r1, r2, r3, r4), (None, s1, s2, s3, s4), d2d, ag
 
         def __init__(self, w):
             self.w, self.id, self.r, self.s, self.f = w, w, mod(w, NRS), mod(w, NDD), mod(w, NX)
@@ -435,7 +493,7 @@
 
     class Short:
         parts = SHORT
-        accumulated, received, sent, crossed, ag_ref = accm, (None, q1, q2, q3, q4, q5, q6), (None, t1, t2, t3, t4, t5, t6), d2dm, agm
+        accumulated, received, sent, crossed, ag_ref = accm, (None, q1, q2, q3, q4), (None, t1, t2, t3, t4), d2dm, agm
 
         def __init__(self, w):
             self.w, self.id, self.r, self.s, self.f = w, NW + w, w, w, NX + w
@@ -446,16 +504,16 @@
 
     def crossing(v):
         s = sems(v)[1]
-        return rcopy(own.at[1 - c, pl.ds(v.own, len(v.parts))], v.crossed.at[v.s], d2s.at[s], d2r.at[s], other)
+        return rcopy(own.at[ONE - c, pl.ds(v.own, len(v.parts))], v.crossed.at[v.s], d2s.at[s], d2r.at[s], other)
 
     def stage_all(v, j):
         s = sems(v)[0]
-        return rcopy(v.sent[j].at[v.r], v.received[j].at[v.r], ssem.at[s, j - 1], rsem.at[s, j - 1], other)
+        return rcopy(v.sent[j].at[v.r], v.received[j].at[v.r], ssem.at[s, j - ONE], rsem.at[s, j - ONE], other)
 
     def stage_one(v, j, k):
         s = sems(v)[0]
-        to = partners[(v.parts[k] + j - 1) % PARTS]
-        return rcopy(v.sent[j].at[v.r, k], v.received[j].at[v.r, k], ssem.at[s, j - 1], rsem.at[s, j - 1], to)
+        to = partners[(v.parts[k] + j - ONE) % PARTS]
+        return rcopy(v.sent[j].at[v.r, k], v.received[j].at[v.r, k], ssem.at[s, j - ONE], rsem.at[s, j - ONE], to)
 
     def acc_at(v, k):
         return (v.r * len(v.parts) + k) * HALF
@@ -480,17 +538,17 @@
         def make(k):
             p = v.parts[k]
             b = bits[p]
-            lv, kp = (1 - b) * TWO ** (PARTS - 1 - p), b * TWO ** (PARTS - 1 - p)
+            lv, kp = (ONE - b) * TWO ** (PARTS - ONE - p), b * TWO ** (PARTS - ONE - p)
             def some(g, _):
-                at_g = rotr(g * OCT, p)
-                for i in range(OCT):
+                at_g = rotr(g * RUN, p)
+                for i in range(RUN):
                     u = at_g + rotr(i, p)
                     both = [own[c, v.own + k, o + u].astype(F32) + v.crossed[v.s, k, o + u].astype(F32) for o in (lv, kp)]
-                    v.sent[1][v.r, k, g * OCT + i] = both[0].astype(BF)
-                    v.accumulated[acc_at(v, k) + g * OCT + i] = both[1]
+                    v.sent[1][v.r, k, g * RUN + i] = both[0].astype(BF)
+                    v.accumulated[acc_at(v, k) + g * RUN + i] = both[1]
                 return 0
 
-            loop(HALF // OCT, some)
+            loop(HALF // RUN, some)
             return stage_one(v, 1, k)
 
         lag_start([functools.partial(make, k) for k in range(len(v.parts))])
@@ -501,18 +559,52 @@
             def _():
                 signal(d2c.at[v.s], other)
 
+    def peer_block(p, e):
+        r = 0
+        for j, bit in zip((3, 4, 5), (4, 2, 1)):
+            own_bit = bits[(p + j) % PARTS]
+            r = TWO * r + (ONE - own_bit if e & bit else own_bit)
+        return r
+
+    def seven(v, ref):
+        s = sems(v)[0]
+        view = ref.at[v.r, :, pl.ds(0, OCT - 1)]
+        return rcopy(view, view, ssem.at[s, 3], rsem.at[s, 3], other)
+
+    def rs4(v):
+        stage_all(v, 3).wait_recv()
+
+        def make(k):
+            p = v.parts[k]
+            o = pl.ds(acc_at(v, k) + kept(p, 3) - kept(p, 1), OCT)
+            total = v.accumulated[o] + v.received[3][v.r, k].astype(F32)
+            v.accumulated[o] = total
+            v.sent[4][v.r, k] = total.astype(BF)
+            s = sems(v)[0]
+            return [
+                rcopy(v.sent[4].at[v.r, k, peer_block(p, e)], v.received[4].at[v.r, k, e - 1], ssem.at[s, 3], rsem.at[s, 3], across[near[p][e - 1]])
+                for e in range(1, OCT)
+            ]
+
+        last = []
+        for k in range(len(v.parts) + 1):
+            made = make(k) if k < len(v.parts) else []
+            for cp in last:
+                cp.start()
+            last = made
+
     def rsj(j, v):
-        stage_all(v, j - 1).wait_recv()
+        stage_all(v, j - ONE).wait_recv()
         n = L(j)
         ch = min(n, OCT)
 
         def make(k):
             p = v.parts[k]
-            b = bits[(p + j - 1) % PARTS]
-            o = acc_at(v, k) + kept(p, j - 1) - kept(p, 1)
+            b = bits[(p + j - ONE) % PARTS]
+            o = acc_at(v, k) + kept(p, j - ONE) - kept(p, 1)
             for i in range(0, n, ch):
-                lv, kp = (1 - b) * n + i, b * n + i
-                both = [v.accumulated[pl.ds(o + h, ch)] + v.received[j - 1][v.r, k, pl.ds(h, ch)].astype(F32) for h in (lv, kp)]
+                lv, kp = (ONE - b) * n + i, b * n + i
+                both = [v.accumulated[pl.ds(o + h, ch)] + v.received[j - ONE][v.r, k, pl.ds(h, ch)].astype(F32) for h in (lv, kp)]
                 v.sent[j][v.r, k, pl.ds(i, ch)] = both[0].astype(BF)
                 v.accumulated[pl.ds(o + kp, ch)] = both[1]
             return stage_one(v, j, k)
@@ -523,17 +615,20 @@
         return (w >= D1) & (w < G0)
 
     def exchange(v):
-        return rcopy(gfin.at[v.f, 1 - c], xg.at[v.id], xs.at[v.f], xr.at[v.id], other)
-
-    def rs7(v):
-        stage_all(v, PARTS).wait_recv()
+        return rcopy(gfin.at[v.f, ONE - c], xg.at[v.id], xs.at[v.f], xr.at[v.id], other)
+
+    def rs5(v):
+        seven(v, v.received[4]).wait_recv()
         for k, p in enumerate(v.parts):
-            g = v.accumulated[acc_at(v, k) + rot[p] - kept(p, 1)] + v.received[PARTS][v.r, k, 0].astype(F32)
+            g = v.accumulated[acc_at(v, k) + rot[p] - kept(p, 1)]
+            for e in range(OCT - 1):
+                g = g + v.received[4][v.r, k, e].astype(F32)
             g = g.astype(BF).astype(F32)
             for h in range(TWO):
                 gfin[v.f, h, k] = g[OCT * h : OCT * h + OCT]
-        for j in range(1, PARTS + 1):
+        for j in range(1, 4):
             stage_all(v, j).wait_send()
+        seven(v, v.sent[4]).wait_send()
         if isinstance(v, Short):
             g_d[v.w, ROWS * UNITS : ROWS * UNITS + OCT] = gfin[v.f, 0, 1]
             exchange(v).start()
@@ -565,7 +660,7 @@
             wsend[v.f, mat, k] = wn
 
     def w_exchange(v):
-        return rcopy(wsend.at[v.f, 1 - c], wrecv.at[v.id], wsm.at[v.f], wrm.at[v.id], other)
+        return rcopy(wsend.at[v.f, ONE - c], wrecv.at[v.id], wsm.at[v.f], wrm.at[v.id], other)
 
     def unless_down(fn):
         def run(v):
@@ -581,7 +676,7 @@
         return run
 
     @unless_down
-    def rs8(v):
+    def rs6(v):
         exchange(v).wait_recv()
         if isinstance(v, Short):
             adam_tile(v.w, 0, v, 0)
@@ -596,7 +691,7 @@
         w_exchange(v).start()
 
     @unless_down
-    def rs9(v):
+    def rs7(v):
         w_exchange(v).wait_recv()
         for k in range(PARTS if isinstance(v, Full) else 1):
             mine, theirs = wsend[v.f, c, k], wrecv[v.id, k]
@@ -675,22 +770,23 @@
         for k, p in enumerate(v.parts):
             src, dst = fin.at[v.id, k], part_of(v).at[k, rot[p]]
             copy(src, dst, agl.at[v.id]).start()
-            rcopy(src, dst, ags.at[v.id], agr.at[v.id, 0], partners[(p + PARTS - 1) % PARTS]).start()
-            rcopy(src, dst, dags.at[v.id], dagr.at[v.id], other).start()
+            for dims in near[p]:
+                rcopy(src, dst, ags.at[v.id], agr.at[v.id, 0], across[dims]).start()
 
     def agk(k, v):
         n = 2 ** (k - 2)
         mine = part_of(v)
-        if k == 2:
+        first = k == 4
+        if first:
             copy(fin.at[v.id, pl.ds(0, len(v.parts))], mine.at[:, 0], agl.at[v.id]).wait()
-        came = mine.at[:, pl.ds(0, n)]
-        rcopy(came, came, ags.at[v.id], agr.at[v.id, k - 2], other).wait_recv()
-        j = PARTS + 1 - k
+        came = mine.at[:, pl.ds(0, OCT - 1 if first else n)]
+        rcopy(came, came, ags.at[v.id], agr.at[v.id, 0 if first else k - 4], other).wait_recv()
+        j = PARTS + ONE - k
         for q, p in enumerate(v.parts):
             if k <= PARTS:
                 h = mine.at[q, pl.ds(kept(p, j), TWO * n)]
-                rcopy(h, h, ags.at[v.id], agr.at[v.id, k - 1], partners[(p + j - 1) % PARTS]).start()
-            g = mine.at[q, pl.ds(kept(p, j) + (1 - bits[(p + j) % PARTS]) * n, n)]
+                rcopy(h, h, ags.at[v.id], agr.at[v.id, k - 3], partners[(p + j - ONE) % PARTS]).start()
+            g = mine.at[q, pl.ds(kept(p, j), OCT) if first else pl.ds(kept(p, j) + (ONE - bits[(p + j) % PARTS]) * n, n)]
             rcopy(g, g, dags.at[v.id], dagr.at[v.id], other).start()
 
     def ag_end(v):
@@ -700,8 +796,8 @@
         cp.wait_send()
         cp.wait_recv()
 
-    rs_stages = [rs0, rs1] + [functools.partial(rsj, j) for j in range(TWO, PARTS + 1)] + [rs7, rs8, rs9]
-    ag_stages = [ag1] + [functools.partial(agk, k) for k in range(TWO, PARTS + 2)] + [ag_end]
+    rs_stages = [rs0, rs1, functools.partial(rsj, 2), functools.partial(rsj, 3), rs4, rs5, rs6, rs7]
+    ag_stages = [ag1] + [functools.partial(agk, k) for k in range(4, PARTS + 2)] + [ag_end]
 
     def find(t, table):
         terms = [jnp.where(t == s, q + 1, 0) for q, s in enumerate(table)]
@@ -709,38 +805,44 @@
             terms = [sum(terms[q : q + 2]) for q in range(0, len(terms), 2)]
         return terms[0]
 
-    def run(fns, offs, s, t, kind, table):
-        w = find(t - offs[s], table)
+    def run(fn, t, kind, ticks):
+        w = find(t, ticks)
 
         @pl.when(w > 0)
         def _():
-            fns[s](kind(w - 1))
-
-    def stages(fns, offs, t, table, short_table):
-        @pl.when((t >= min(table)) & (t <= max(table) + offs[-1]))
-        def _():
+            fn(kind(w - 1))
+
+    def within(t, ticks, fn):
+        pl.when((t >= min(min(ticks))) & (t <= max(max(ticks))))(fn)
+
+    def stages(fns, t, full, short):
+        full, short = tuple(zip(*full)), tuple(zip(*short))
+
+        def full_ones():
             for odd in range(TWO):
 
                 @pl.when(mod(t, 2) == odd)
                 def _():
-                    for s in reversed(range(len(offs))):
-                        if (offs[s] + 1) % TWO == odd:
-                            run(fns, offs, s, t, Full, table)
-
-        @pl.when((t >= min(short_table)) & (t <= max(short_table) + offs[-1]))
-        def _():
-            for s in reversed(range(len(offs))):
-                run(fns, offs, s, t, Short, short_table)
+                    for fn, due in zip(reversed(fns), reversed(full)):
+                        if due[0] % TWO == odd:
+                            run(fn, t, Full, due)
+
+        def short_ones():
+            for fn, due in zip(reversed(fns), reversed(short)):
+                run(fn, t, Short, due)
+
+        within(t, full, full_ones)
+        within(t, short, short_ones)
 
     def moves(t):
-        stages(rs_stages, OFF, t, START, SHORT_START)
+        stages(rs_stages, t, RS_TICKS, SHORT_RS_TICKS)
         for q, fn in enumerate((dx1, dx2, dx3)):
 
             @pl.when((t == DX[0][q]) | (t == DX[1][q]))
             def _():
                 fn(jnp.where(t == DX[1][q], 1, 0))
 
-        stages(ag_stages, AGO, t, AGS, SHORT_AGS)
+        stages(ag_stages, t, AG_TICKS, SHORT_AG_TICKS)
 
     loads = [copy(x, acts.at[2], lsem.at[1]), copy(dy, acts.at[0], lsem.at[2])]
     rows_in = [copy(w.at[:, aligned(dp * OCT, OCT)], o, lsem.at[3 + k]) for k, (w, o) in enumerate(((w_gate, wr_g), (w_up, wr_u)))]
@@ -770,13 +872,13 @@
 def step_call(args):
     B = (ROWS, LANES)
     V, R, S = pltpu.VMEM, pltpu.SemaphoreType.REGULAR, pltpu.SemaphoreType.DMA
-    sizes = [TWO**k for k in reversed(range(PARTS))]
+    sizes = [HALF, HALF // TWO, OCT, OCT]
     n, ns = NW + NS, len(SHORT)
     own_parts = OWN_SLOTS * PARTS + NS * ns
     E = (PARTS, OCT, LANES)
     scratch = [
         V((3, TOK, D), BF), V((D, TOK), BF), V((4 * TB, *B), F32), V((TWO, D, TWO * TILE), BF), V((TWO, TILE, D), BF),
-        V((TOK, TWO * TILE), BF), V((TOK, TILE), BF), V((TWO, TILE, TOK), BF), V((TWO, PAIR, TOK), BF),
+        V((TWO, TOK, TWO * TILE), BF), V((TOK, TILE), BF), V((TWO, TILE, TOK), BF), V((TWO, PAIR, TOK), BF),
         *[V((LAYERS, OCT, FF), BF)] * TWO, V((LAYERS, WIN, D), BF), *[V((OWN_ROWS, LAYERS, D), F32)] * TWO,
         V((TWO, own_parts, CHIPS, *B), BF), V((NDD, PARTS, CHIPS, *B), BF), V((NRS * PARTS * HALF, *B), F32),
         *[V((NRS, PARTS, k, *B), BF) for k in sizes * TWO],
@@ -784,18 +886,18 @@
         *[V((NS, ns, k, *B), BF) for k in sizes * TWO],
         V((NX + NS, TWO, *E), F32), V((n, *E), F32), V((NX + NS, TWO, *E), F32), V((n, *E), F32), V((n, PARTS, *B), BF),
         V((LAYERS, ROWS * (UNITS + 1), LANES), F32), *[V((LAYERS, GROUP, WIN, LANES), F32)] * 3,
-        S((12,)), S((TWO, 3)), S((TWO,)), S((TWO, 2)), S((TWO,)), S((NDD + NS,)), S((NDD + NS,)), S((NRS + NS, PARTS)), S((NRS + NS, PARTS)),
+        S((12,)), S((TWO, 3)), S((TWO,)), S((TWO,)), S((TWO, 2)), S((TWO,)), S((NDD + NS,)), S((NDD + NS,)), S((NRS + NS, PARTS)), S((NRS + NS, PARTS)),
         S((NX + NS,)), S((n,)), S((NX + NS,)), S((n,)), S((n,)), S((n,)), S((n, PARTS)), S((n,)), S((n,)), S((TWO, LAYERS)), S((TWO, LAYERS)),
         R((NDD,)), R((NRS,)),
     ]
     hbm, vmem = pl.BlockSpec(memory_space=pl.ANY), pl.BlockSpec(memory_space=pltpu.VMEM)
-    out = [((NW, TWO, PARTS, CHIPS, *B), BF), ((NS, 2, ns, CHIPS, *B), BF), ((LAYERS, FF, TOK), BF), ((D, TOK), BF), ((TILES, TWO * TB, *B), F32)]
+    out = [((NW, TWO, PARTS, CHIPS, *B), BF), ((NS, 2, ns, CHIPS, *B), BF), ((LAYERS, FF, TOK), BF), ((D, TOK), BF), ((TILES, TWO * TB, *B), F32), ((TILES, TOK, TWO * TILE), BF)]
     out += [(s, F32) for s in ((LAYERS, OCT, FF), (LAYERS, OCT, FF), (LAYERS, WIN, D))] * TWO
     return pl.pallas_call(
         step_kernel,
         out_shape=[jax.ShapeDtypeStruct(*o) for o in out],
         in_specs=[hbm] * 11,
-        out_specs=[hbm] * 5 + [vmem] * 6,
+        out_specs=[hbm] * 6 + [vmem] * 6,
         scratch_shapes=scratch,
         compiler_params=pltpu.CompilerParams(collective_id=0, has_side_effects=True, vmem_limit_bytes=67043328),
         name="step",
@@ -811,10 +913,10 @@
     outs = (gate, up)
 
     def load(k):
-        return copy(ag.at[jnp.where(k < D1, k, k + D1)], buf.at[mod(k, 2)], isem.at[mod(k, 2)])
+        return copy(ag.at[jnp.where(k < D1, k, k + D1)], buf.at[mod(k, DEEP)], isem.at[mod(k, DEEP)])
 
     def stores(k):
-        cols = aligned(LANES + PARTS * LANES * (mod(k, 4)), PARTS * LANES, LANES)
+        cols = aligned(LANES + PARTS * LANES * mod(k, 4), PARTS * LANES, LANES)
         return [copy(stage.at[mod(k, 2), m], o.at[jnp.where(k < D1, 1, 0), :, cols], osem.at[mod(k, 2), m]) for m, o in enumerate(outs)]
 
     def load_down(layer):
@@ -828,49 +930,58 @@
         return copy(mstage.at[layer, m], outs[m].at[layer, :, lanes(0)], mosem.at[layer, m])
 
     mini = copy(agm, mbuf, msem.at[0])
-    for cp in (load_down(1), mini, load(0), load_down(0)):
+    for cp in (load(0), load(1), load_down(1), mini, load(2), load_down(0)):
         cp.start()
-    for o, t in ((pm_g, om_g), (pm_u, om_u), (pv_g, ov_g), (pv_u, ov_u)):
-        o[...] = t[...]
-    for o, t in ((pm_d, om_d), (pv_d, ov_d)):
-        for layer in range(LAYERS):
-            for r in range(OWN_ROWS):
-                o[r, layer : layer + 1] = t[layer, r : r + 1]
-    mini.wait()
 
     def by_chip(dst, cols, src, p):
         for u in range(CHIPS):
             n = CHIP_AT[u]
             dst[ROWS * n : ROWS * n + ROWS, cols] = src[rotl(u, p)]
 
-    for layer in range(LAYERS):
-        for m in range(TWO):
-            by_chip(mstage.at[layer, m], lanes(0), mbuf.at[layer, m, 0], SHORT[0])
-            store_short(layer, m).start()
-
     def body(k, _):
+        @pl.when(k < jobs)
+        def _():
+            load(k).wait()
+
+            @pl.when(k >= 2)
+            def _():
+                for cp in stores(k - 2):
+                    cp.wait()
+
+            for m in range(TWO):
+                for p in range(PARTS):
+                    by_chip(stage.at[mod(k, 2), m], lanes(p), buf.at[mod(k, DEEP), m, p], p)
+            for cp in stores(k):
+                cp.start()
+
+            @pl.when(k + DEEP < jobs)
+            def _():
+                load(k + DEEP).start()
+
+        @pl.when(k >= 1)
+        def _():
+            down_job(k - ONE)
+
+        return 0
+
+    def down_job(k):
         layer = jnp.where(k < D1, 1, 0)
 
+        @pl.when(k == 0)
+        def _():
+            mini.wait()
+            for layer in range(LAYERS):
+                for m in range(TWO):
+                    by_chip(mstage.at[layer, m], lanes(0), mbuf.at[layer, m, 0], SHORT[0])
+                    store_short(layer, m).start()
+
         @pl.when(mod(k, 4) == 0)
         def _():
             load_down(layer).wait()
 
-        load(k).wait()
-
-        @pl.when(k + 1 < jobs)
-        def _():
-            load(k + 1).start()
-
         @pl.when(k >= 2)
         def _():
-            for cp in stores(k - 2) + [store_down(k - 2)]:
-                cp.wait()
-
-        for m in range(TWO):
-            for p in range(PARTS):
-                by_chip(stage.at[mod(k, 2), m], lanes(p), buf.at[mod(k, 2), m, p], p)
-        for cp in stores(k):
-            cp.start()
+            store_down(k - 2).wait()
 
         def pair(q, _):
             for lt in range(OCT):
@@ -890,9 +1001,17 @@
 
         loop(2, pair)
         store_down(k).start()
-        return 0
-
-    loop(jobs, body)
+
+        @pl.when(k == jobs - 1)
+        def _():
+            for o, t in ((pm_g, om_g), (pm_u, om_u), (pv_g, ov_g), (pv_u, ov_u)):
+                o[...] = t[...]
+            for o, t in ((pm_d, om_d), (pv_d, ov_d)):
+                for layer in range(LAYERS):
+                    for r in range(OWN_ROWS):
+                        o[r, layer : layer + 1] = t[layer, r : r + 1]
+
+    loop(jobs + 1, body)
     for k in (jobs - 2, jobs - 1):
         for cp in stores(k) + [store_down(k)]:
             cp.wait()
@@ -913,9 +1032,9 @@
         in_specs=[hbm] * TWO + [vmem] * 6,
         out_specs=[hbm] * 3 + [vmem] * 6,
         scratch_shapes=[
-            V((TWO, *whole), BF), V((LAYERS, TWO, *whole), BF), V((NS, 2, len(SHORT), CHIPS, ROWS, LANES), BF),
+            V((DEEP, *whole), BF), V((LAYERS, TWO, *whole), BF), V((NS, 2, len(SHORT), CHIPS, ROWS, LANES), BF),
             V((TWO, TWO, D, PARTS * LANES), BF), V((LAYERS, TWO, D, LANES), BF), V((TWO, TWO * PAIR, D), BF),
-            S((TWO,)), S((TWO,)), S((1,)), S((TWO, 2)), S((TWO, 2)), S((TWO,)),
+            S((DEEP,)), S((TWO,)), S((1,)), S((TWO, 2)), S((TWO, 2)), S((TWO,)),
         ],
         compiler_params=pltpu.CompilerParams(vmem_limit_bytes=60 * TWO**20),
         name="place",
@@ -924,7 +1043,7 @@
 
 def local_step(x, dy, w_gate, w_up, w_down, m_g, m_u, m_d, v_g, v_u, v_d):
     m_d, v_d = (jnp.transpose(t, (1, 0, 2)) for t in (m_d, v_d))
-    ag, agm, _, _, _, *moments = step_call((x[0], dy[0], w_gate, w_up, w_down, m_g, m_u, m_d, v_g, v_u, v_d))
+    ag, agm, _, _, _, _, *moments = step_call((x[0], dy[0], w_gate, w_up, w_down, m_g, m_u, m_d, v_g, v_u, v_d))
     gate, up, down, om_g, om_u, om_d, ov_g, ov_u, ov_d = place_call((ag, agm, *moments))
     om_d, ov_d = (jnp.transpose(t, (1, 0, 2)) for t in (om_d, ov_d))
     return gate, up, down, om_g, om_u, om_d, ov_g, ov_u, ov_d

time: 338 us -> 313 us (0.926)
  Pallas kernels: 336 us -> 312 us
    pallas_call x1, Pallas kernels: 305 us -> 284 us  [step_call(): pl.pallas_call(step_kernel, out_shape=[jax.ShapeDtypeStruct(*o) for o in...]
    pallas_call x1, Pallas kernels: 31.8 us -> 27.6 us  [place_call(): pl.pallas_call(place_kernel, out_shape=[jax.ShapeDtypeStruct(*o) for o in...]
where the time goes in v3:
time: 313 us; the launch traced here: 312 us
  Pallas kernels  312 us (100%)
    pallas_call x1, Pallas kernels, step_call(): pl.pallas_call(step_kernel, out_shape=[jax.ShapeDtypeStruct(*o) for o in...  284 us
    pallas_call x1, Pallas kernels, place_call(): pl.pallas_call(place_kernel, out_shape=[jax.ShapeDtypeStruct(*o) for o in...  27.6 us

profile of v3, /device:TPU:1, one launch (start us, length us, event | category | flops | bytes accessed | tf_op | source)
XLA Modules:
  0.0 312.5 jit_solution(15252193022428242769)
XLA Ops:
  0.6 284.2 %step.1 = (bf16[12,2,6,64,16,128]{5,4,3,2,1,0:T(8,128)(2,1)}, bf16[2,2,2,64,16,128]{5,4,3,2,1,0:T(8,128)(2,1)}, bf16[2,3200,1024]{2,1,0:T(8,128)(2,1)}, bf16[102...) custom-call(bf16[1024,1024]{1,0:T(8,128)(2,1)} %bitcast.6, ...), custom_call_target="tpu_custom_call" | custom-call | tf_op jit(solution)/shard_map/step/pallas_call | solution.py:896
  284.8 27.6 %place.1 = (bf16[2,1024,3200]{2,1,0:T(8,128)(2,1)}, bf16[2,1024,3200]{2,1,0:T(8,128)(2,1)}, bf16[2,3200,1024]{2,1,0:T(8,128)(2,1)}, f32[2,8,3200]{2,1,0:T(8,128)...) custom-call(bf16[12,2,6,64,16,128]{5,4,3,2,1,0:T(8,128)(2,1)} %get-t, ...), custom_call_target="tpu_custom_call" | custom-call | tf_op jit(solution)/shard_map/place/pallas_call | solution.py:1029

commit v4 on v3

--- a/solution.py
+++ b/solution.py
@@ -39,11 +39,11 @@
     return tuple(tuple(accumulate((ord(ch) - ord("0") for ch in code), initial=20))[1:] for code in codes)
 
 
-RS_TICKS = ticks(('34427211', '74623257', '=4421211', 'C4223211', 'G2241417', 'K422521=', 'S2221271', 'U422143;', 'W4223433', '[2243473', ']6421831', 'a6263411'))
-SHORT_RS_TICKS = ticks(('T2221693', 'I1242751'))
-AG_TICKS = ticks(('J34;>A', 'Z96SP7', 'L343TE', 'T56=DM', '^A49>7', '`7:3JA', 'h;D9:C', 'p9:A@A', 'l;8?:3', 't9F?85', 'vC6I:9', 'x=L5:9'))
-SHORT_AG_TICKS = ticks(('q6@@G9', 't=E>;;'))
-DX = ticks(('e12', 'Z12'))
+RS_TICKS = ticks(('14322411', '74322211', '=4322211', 'C2322411', 'G2322211', 'I2322211', 'S2322211', 'U2322211', 'W2322611', '[4344411', ']4544411', 'a6362411'))
+SHORT_RS_TICKS = ticks(('T2321211', 'G2322212'))
+AG_TICKS = ticks(('B23234', 'F23432', 'L43254', 'R23432', 'Z23472', '\\45654', 'n47674', 'j63652', 'h63454', 'p43654', 't45656', 'x45474'))
+SHORT_AG_TICKS = ticks(('j43441', 'Z23731'))
+DX = ticks(('`64', 'T33'))
 TICKS = max(max(t) for t in AG_TICKS + SHORT_AG_TICKS) + 1
 
 
@@ -662,20 +662,6 @@
     def w_exchange(v):
         return rcopy(wsend.at[v.f, ONE - c], wrecv.at[v.id], wsm.at[v.f], wrm.at[v.id], other)
 
-    def unless_down(fn):
-        def run(v):
-            if isinstance(v, Short):
-                fn(v)
-            else:
-
-                @pl.when(~is_down(v.w))
-                def _():
-                    fn(v)
-
-        run.__name__ = fn.__name__
-        return run
-
-    @unless_down
     def rs6(v):
         exchange(v).wait_recv()
         if isinstance(v, Short):
@@ -690,7 +676,6 @@
         exchange(v).wait_send()
         w_exchange(v).start()
 
-    @unless_down
     def rs7(v):
         w_exchange(v).wait_recv()
         for k in range(PARTS if isinstance(v, Full) else 1):
@@ -799,40 +784,40 @@
     rs_stages = [rs0, rs1, functools.partial(rsj, 2), functools.partial(rsj, 3), rs4, rs5, rs6, rs7]
     ag_stages = [ag1] + [functools.partial(agk, k) for k in range(4, PARTS + 2)] + [ag_end]
 
-    def find(t, table):
-        terms = [jnp.where(t == s, q + 1, 0) for q, s in enumerate(table)]
+    def find(t, due):
+        terms = [jnp.where(t == s, w + 1, 0) for w, s in due]
         while len(terms) > 1:
             terms = [sum(terms[q : q + 2]) for q in range(0, len(terms), 2)]
         return terms[0]
 
-    def run(fn, t, kind, ticks):
-        w = find(t, ticks)
-
-        @pl.when(w > 0)
-        def _():
-            fn(kind(w - 1))
-
-    def within(t, ticks, fn):
-        pl.when((t >= min(min(ticks))) & (t <= max(max(ticks))))(fn)
+    def within(t, due, fn):
+        at = [s for _, s in due]
+        pl.when((t >= min(at)) & (t <= max(at)))(fn)
+
+    def run(t, kind, some):
+        found = [(fn, find(t, due)) for fn, due in reversed(some)]
+
+        @pl.when(sum(w for _, w in found) > 0)
+        def _():
+            for fn, w in found:
+
+                @pl.when(w > 0)
+                def _():
+                    fn(kind(w - 1))
 
     def stages(fns, t, full, short):
-        full, short = tuple(zip(*full)), tuple(zip(*short))
+        full = [[(w, at[s]) for w, at in enumerate(full) if not (fn in (rs6, rs7) and is_down(w))] for s, fn in enumerate(fns)]
+        short = [[(w, at[s]) for w, at in enumerate(short)] for s in range(len(fns))]
 
         def full_ones():
             for odd in range(TWO):
 
                 @pl.when(mod(t, 2) == odd)
                 def _():
-                    for fn, due in zip(reversed(fns), reversed(full)):
-                        if due[0] % TWO == odd:
-                            run(fn, t, Full, due)
-
-        def short_ones():
-            for fn, due in zip(reversed(fns), reversed(short)):
-                run(fn, t, Short, due)
-
-        within(t, full, full_ones)
-        within(t, short, short_ones)
+                    run(t, Full, [(fn, due) for fn, due in zip(fns, full) if due[0][1] % TWO == odd])
+
+        within(t, sum(full, []), full_ones)
+        within(t, sum(short, []), lambda: run(t, Short, list(zip(fns, short))))
 
     def moves(t):
         stages(rs_stages, t, RS_TICKS, SHORT_RS_TICKS)
@@ -862,7 +847,7 @@
     pl.semaphore_wait(barrier, GROUP - 1 + len(far))
 
     def tick(t, _):
-        compute(t)
+        pl.when(t < T_TAIL)(lambda: compute(t))
         moves(t)
         return 0
 

time: 313 us -> 302 us (0.965)
  Pallas kernels: 312 us -> 300 us
    pallas_call x1, Pallas kernels: 284 us -> 273 us  [step_call(): pl.pallas_call(step_kernel, out_shape=[jax.ShapeDtypeStruct(*o) for o in...]
where the time goes in v4:
time: 302 us; the launch traced here: 301 us
  Pallas kernels  300 us (99%)
    pallas_call x1, Pallas kernels, step_call(): pl.pallas_call(step_kernel, out_shape=[jax.ShapeDtypeStruct(*o) for o in...  273 us
    pallas_call x1, Pallas kernels, place_call(): pl.pallas_call(place_kernel, out_shape=[jax.ShapeDtypeStruct(*o) for o in...  27.6 us

profile of v4, /device:TPU:1, one launch (start us, length us, event | category | flops | bytes accessed | tf_op | source)
XLA Modules:
  0.0 300.9 jit_solution(933008753877111054)
XLA Ops:
  0.6 272.6 %step.1 = (bf16[12,2,6,64,16,128]{5,4,3,2,1,0:T(8,128)(2,1)}, bf16[2,2,2,64,16,128]{5,4,3,2,1,0:T(8,128)(2,1)}, bf16[2,3200,1024]{2,1,0:T(8,128)(2,1)}, bf16[102...) custom-call(bf16[1024,1024]{1,0:T(8,128)(2,1)} %bitcast.6, ...), custom_call_target="tpu_custom_call" | custom-call | tf_op jit(solution)/shard_map/step/pallas_call | solution.py:881
  273.3 27.6 %place.1 = (bf16[2,1024,3200]{2,1,0:T(8,128)(2,1)}, bf16[2,1024,3200]{2,1,0:T(8,128)(2,1)}, bf16[2,3200,1024]{2,1,0:T(8,128)(2,1)}, f32[2,8,3200]{2,1,0:T(8,128)...) custom-call(bf16[12,2,6,64,16,128]{5,4,3,2,1,0:T(8,128)(2,1)} %get-t, ...), custom_call_target="tpu_custom_call" | custom-call | tf_op jit(solution)/shard_map/place/pallas_call | solution.py:1014

commit v5 on v4

--- a/solution.py
+++ b/solution.py
@@ -22,7 +22,7 @@
 UNITS = ROWS_GROUP // ROWS
 OWN_ROWS = ROWS_GROUP // GROUP
 WIN = 32
-RUN = 16
+RUN = 32
 DEEP = 3
 
 G1, D1, D0, G0, NW = 0, 4, 6, 8, 12
@@ -36,14 +36,14 @@
 
 
 def ticks(codes):
-    return tuple(tuple(accumulate((ord(ch) - ord("0") for ch in code), initial=20))[1:] for code in codes)
-
-
-RS_TICKS = ticks(('14322411', '74322211', '=4322211', 'C2322411', 'G2322211', 'I2322211', 'S2322211', 'U2322211', 'W2322611', '[4344411', ']4544411', 'a6362411'))
-SHORT_RS_TICKS = ticks(('T2321211', 'G2322212'))
-AG_TICKS = ticks(('B23234', 'F23432', 'L43254', 'R23432', 'Z23472', '\\45654', 'n47674', 'j63652', 'h63454', 'p43654', 't45656', 'x45474'))
-SHORT_AG_TICKS = ticks(('j43441', 'Z23731'))
-DX = ticks(('`64', 'T33'))
+    return tuple(tuple(accumulate((ord(ch) - ord("0") for ch in code), initial=18))[1:] for code in codes)
+
+
+RS_TICKS = ticks(('34322411', '94322211', '?4322211', 'E2322411', 'I2322211', 'K2322211', 'U2322211', 'W2322211', 'Y2324411', ']4344211', '_4542411', 'c6342411'))
+SHORT_RS_TICKS = ticks(('V2321211', 'I2322212'))
+AG_TICKS = ticks(('D23234', 'H23432', 'N43254', 'T23432', '\\23452', '^45634', 'n47674', 'l43652', 'j43454', 'p43654', 't45654', 'x45454'))
+SHORT_AG_TICKS = ticks(('l23441', ']25551'))
+DX = ticks(('b64', 'V33'))
 TICKS = max(max(t) for t in AG_TICKS + SHORT_AG_TICKS) + 1
 
 
@@ -271,10 +271,10 @@
 
     def by_rows(fn):
         def chunk(k, _):
-            fn(k * LANES, aligned(k * LANES, LANES))
+            fn(k * TILE, aligned(k * TILE, TILE))
             return 0
 
-        loop(TOK // LANES, chunk)
+        loop(TOK // TILE, chunk)
 
     def norm_in(_, rows):
         h = acts[2, rows].astype(F32)
@@ -285,10 +285,10 @@
             gu_out(TILES - 2 + (b + TILES) % TWO, b).wait()
 
         def chunk(r, rows):
-            o = jnp.concatenate([get_da(q, r, LANES) for q in range(OCT)], 1).astype(BF).astype(F32)
+            o = jnp.concatenate([get_da(q, r, TILE) for q in range(OCT)], 1).astype(BF).astype(F32)
             acts[2, rows] = (acts[2, rows].astype(F32) + o).astype(BF)
             for q in range(OCT):
-                da[pl.ds(q * CHIPS + div(r, ROWS), OCT)] = jnp.zeros((OCT, ROWS, LANES), F32)
+                da[pl.ds(q * CHIPS + div(r, ROWS), ROWS)] = jnp.zeros((ROWS, ROWS, LANES), F32)
             norm_in(r, rows)
 
         by_rows(chunk)
@@ -385,7 +385,7 @@
     def tick_norm():
         def chunk(r, rows):
             h = acts[2, rows].astype(F32)
-            g = jnp.concatenate([get_da(q, r, LANES) for q in range(OCT)], 1).astype(BF).astype(F32)
+            g = jnp.concatenate([get_da(q, r, TILE) for q in range(OCT)], 1).astype(BF).astype(F32)
             scale = rms_scale(jnp.sum(h * h, -1, keepdims=True))
             back = scale * scale * scale * jnp.sum(h * g, -1, keepdims=True) * (1.0 / D)
             dh = (g * scale - h * back).astype(BF).astype(F32)
@@ -426,7 +426,8 @@
             for cp in weights(1, 0, 0):
                 cp.start()
             tick_fn()
-            loads[1].wait()
+            for cp in [loads[1], *rows_in]:
+                cp.wait()
 
         @pl.when((t >= T_L1) & (t < T_DOWN1) & (mod(t, 2) == T_L1 % TWO))
         def _():
@@ -548,7 +549,7 @@
                     v.accumulated[acc_at(v, k) + g * RUN + i] = both[1]
                 return 0
 
-            loop(HALF // RUN, some)
+            some(0, None)
             return stage_one(v, 1, k)
 
         lag_start([functools.partial(make, k) for k in range(len(v.parts))])
@@ -834,16 +835,16 @@
     rows_in.append(copy(w_down.at[:, aligned(div(OWN_ROWS * dp, OCT) * OCT, WIN, OCT)], wr_d, lsem.at[5]))
     moments = ((m_g, om_g), (m_u, om_u), (m_d, md), (v_g, ov_g), (v_u, ov_u), (v_d, vd))
     rows_in += [copy(m, o, lsem.at[6 + k]) for k, (m, o) in enumerate(moments)]
-    for cp in loads + weights(0, 0, 0) + rows_in:
+    for cp in [loads[0], *weights(0, 0, 0)]:
         cp.start()
     for q in range(OCT):
         da[pl.ds(q * CHIPS, CHIPS)] = jnp.zeros((CHIPS, ROWS, LANES), F32)
     loads[0].wait()
+    for cp in [loads[1], *rows_in]:
+        cp.start()
     by_rows(norm_in)
     transpose_in()
     a0t_out.start()
-    for cp in rows_in:
-        cp.wait()
     pl.semaphore_wait(barrier, GROUP - 1 + len(far))
 
     def tick(t, _):

time: 302 us -> 300 us (level)
  no operation moved by 1% of the time
where the time goes in v5:
time: 300 us; the launch traced here: 299 us
  Pallas kernels  299 us (100%)
    pallas_call x1, Pallas kernels, step_call(): pl.pallas_call(step_kernel, out_shape=[jax.ShapeDtypeStruct(*o) for o in...  271 us
    pallas_call x1, Pallas kernels, place_call(): pl.pallas_call(place_kernel, out_shape=[jax.ShapeDtypeStruct(*o) for o in...  27.6 us

profile of v5, /device:TPU:1, one launch (start us, length us, event | category | flops | bytes accessed | tf_op | source)
XLA Modules:
  0.0 299.2 jit_solution(105154788697386284)
XLA Ops:
  0.6 270.9 %step.1 = (bf16[12,2,6,64,16,128]{5,4,3,2,1,0:T(8,128)(2,1)}, bf16[2,2,2,64,16,128]{5,4,3,2,1,0:T(8,128)(2,1)}, bf16[2,3200,1024]{2,1,0:T(8,128)(2,1)}, bf16[102...) custom-call(bf16[1024,1024]{1,0:T(8,128)(2,1)} %bitcast.6, ...), custom_call_target="tpu_custom_call" | custom-call | tf_op jit(solution)/shard_map/step/pallas_call | solution.py:882
  271.5 27.6 %place.1 = (bf16[2,1024,3200]{2,1,0:T(8,128)(2,1)}, bf16[2,1024,3200]{2,1,0:T(8,128)(2,1)}, bf16[2,3200,1024]{2,1,0:T(8,128)(2,1)}, f32[2,8,3200]{2,1,0:T(8,128)...) custom-call(bf16[12,2,6,64,16,128]{5,4,3,2,1,0:T(8,128)(2,1)} %get-t, ...), custom_call_target="tpu_custom_call" | custom-call | tf_op jit(solution)/shard_map/place/pallas_call | solution.py:1015
